TPU v7x, 32 devices: a whole 2x2x4 slice. The times are simulated.
32 devices in a mesh: clips: 2 (over y), ha: 4 (over z), ta: 2 (over x), wa: 2 (over core).
Axes of the slice: x: 2, y: 2, z: 4, core: 2. Of those that a mesh axis runs over, the one named last changes fastest.
Arguments:
- frames: bfloat16 [8, 16, 128, 192], P(('clips', 'ta'), 'ha', 'wa'), parts along dimension 0, may hold values from -6 to 6
- cache: bfloat16 [4, 16, 128, 192], P('clips', 'ha', 'wa'), parts along dimension 0, may hold values from -5 to 5
- norm_gain: float32 [192], replicated, may hold values from 0.25 to 1.75
- conv_weight: bfloat16 [3, 3, 3, 192, 192], replicated, may hold values from -0.078125 to 0.078125
- conv_bias: float32 [192], replicated, may hold values from -3 to 3
- up_weight: bfloat16 [3, 3, 192, 96], replicated, may hold values from -0.15625 to 0.15625
- up_bias: float32 [96], replicated, may hold values from -3 to 3
Outputs:
- upsampled: bfloat16 [8, 32, 128, 192], P(('clips', 'ta'), 'ha', 'wa'), parts along dimension 0
There are 2 independent parts, one for each index of `clips`. A program takes and returns all parts, laid end to end along the dimension named above; an argument that names none is the same for every part. Nothing has to cross between parts.
All inputs are finite; a program needn't handle non-finite values.
Results may differ from a plain program's by a relative error of at most 0.0075.
Values may be sent and summed in bfloat16 or wider, within the bound.
No kernel may reach another device: no remote copies, remote signals or barrier semaphores. Data moves between devices by JAX's collectives and lax.ppermute only.
A program may use at most 64 MiB of HBM per device.

v0:
```python
import jax
import jax.numpy as jnp
from jax import lax
from jax.sharding import PartitionSpec as P

EPS = 1e-06
PHASE_TAPS = (((0, (0,)), (1, (1, 2))), ((1, (0, 1)), (2, (2,))))


def shifted(shard, axis, by):
    devices = lax.axis_size(axis)
    pairs = [(i, i + by) for i in range(devices) if 0 <= i + by < devices]
    return lax.ppermute(shard, axis, pairs)


def padded_2(cells, sides, width):
    for axis, dim in sides:
        count = lax.axis_size(axis)
        ends = count - 1
        head = lax.slice_in_dim(cells, 0, width, axis=dim)
        tail = lax.slice_in_dim(cells, cells.shape[dim] - width, cells.shape[dim], axis=dim)
        cells = jnp.concatenate(
            [
                lax.ppermute(tail, axis, [(i, (i + 1) % count) for i in range(ends)]),
                cells,
                lax.ppermute(head, axis, [((i + 1) % count, i) for i in range(ends)]),
            ],
            axis=dim,
        )
    return cells


def activate(values, gain):
    wide = values.astype(jnp.float32)
    scale = lax.rsqrt(jnp.mean(wide * wide, axis=-1, keepdims=True) + EPS)
    return jax.nn.silu(wide * scale * gain).astype(jnp.bfloat16)


def causal_conv(padded, weight, count, rows, cols):
    channels = padded.shape[-1]
    total = jnp.zeros((count * rows * cols, weight.shape[-1]), jnp.float32)
    for a in range(3):
        for b in range(3):
            for c in range(3):
                window = padded[a : a + count, b : b + rows, c : c + cols].reshape(-1, channels)
                total = total + jnp.dot(window, weight[a, b, c], preferred_element_type=jnp.float32)
    return total.reshape(count, rows, cols, -1)


def upsample_conv(bordered, weight, bias):
    count = bordered.shape[0]
    rows = bordered.shape[1] - 2
    cols = bordered.shape[2] - 2
    channels = bordered.shape[-1]
    outputs = weight.shape[-1]
    row_phases = []
    for row_phase in range(2):
        col_phases = []
        for col_phase in range(2):
            total = jnp.zeros((count * rows * cols, outputs), jnp.float32)
            for row_start, row_taps in PHASE_TAPS[row_phase]:
                for col_start, col_taps in PHASE_TAPS[col_phase]:
                    window = bordered[
                        :, row_start : row_start + rows, col_start : col_start + cols
                    ].reshape(-1, channels)
                    if len(row_taps) * len(col_taps) == 1:
                        total = total + jnp.dot(
                            window,
                            weight[row_taps[0], col_taps[0]],
                            preferred_element_type=jnp.float32,
                        )
                    else:
                        folded = jnp.zeros((channels, outputs), jnp.float32)
                        for a in row_taps:
                            for b in col_taps:
                                folded = folded + weight[a, b].astype(jnp.float32)
                        upper = folded.astype(jnp.bfloat16)
                        lower = (folded - upper.astype(jnp.float32)).astype(jnp.bfloat16)
                        total = total + jnp.dot(window, upper, preferred_element_type=jnp.float32)
                        total = total + jnp.dot(window, lower, preferred_element_type=jnp.float32)
            result = (total + bias).astype(jnp.bfloat16)
            col_phases.append(result.reshape(count, rows, cols, outputs))
        row_phases.append(jnp.concatenate(col_phases, axis=-1))
    stacked = jnp.stack(row_phases, axis=2)
    return stacked.reshape(count, 2 * rows, cols, 2 * outputs)


def on_device(frames, cache, norm_gain, conv_weight, conv_bias, up_weight, up_bias):
    count, rows, cols, channels = frames.shape
    activated = activate(frames, norm_gain)
    earlier = shifted(activated, "ta", 1)
    earlier = jnp.where(lax.axis_index("ta") == 0, cache, earlier)
    extended = jnp.concatenate([earlier, activated], axis=0)
    padded = padded_2(extended, (("ha", 1), ("wa", 2)), 1)
    convolved = causal_conv(padded, conv_weight, count, rows, cols)
    residual = (frames.astype(jnp.float32) + convolved + conv_bias).astype(jnp.bfloat16)
    bordered = padded_2(residual, (("ha", 1), ("wa", 2)), 1)
    return upsample_conv(bordered, up_weight, up_bias)


def solution(mesh):
    return jax.shard_map(
        on_device,
        mesh=mesh,
        in_specs=(
            P(("clips", "ta"), "ha", "wa", None),
            P("clips", "ha", "wa", None),
            P(),
            P(),
            P(),
            P(),
            P(),
        ),
        out_specs=P(("clips", "ta"), "ha", "wa", None),
        check_vma=False,
    )
```

profile of v0, /device:TPU:0, one launch (start us, length us, event | category | flops | bytes accessed | tf_op | source)
XLA Modules:
  0.0 61.0 jit_solution(4402095644396140259)
XLA Ops:
  0.0 1.1 %fusion.14 = f32[2,4,64]{2,1,0:T(4,128)S(1)} fusion(bf16[2,4,64,192]{3,2,1,0:T(8,128)(2,1)} %param.7), kind=kLoop, calls=%fused_computation.65 | loop fusion | flops 294400 | bytes 198656 | tf_op jit(solution)/shard_map/reduce_sum | solution.py:35
  1.1 1.2 %fusion.21 = bf16[2,4,64,192]{3,2,1,0:T(8,128)(2,1)S(1)} fusion(bf16[2,4,64,192]{3,2,1,0:T(8,128)(2,1)} %param.7, f32[192]{0:T(256)} %param.9, f32[2,4,64]{2,1,0:T(4,128)S(1)} %add_rsqrt_fusion), kind=kLoop, calls=%fused_computation.72 | loop fusion | flops 786432 | bytes 396032 | tf_op jit(solution)/shard_map/convert_element_type | solution.py:36
  2.3 4.9 %collective-permute-start = (bf16[2,4,64,192]{3,2,1,0:T(8,128)(2,1)S(1)}, bf16[2,4,64,192]{3,2,1,0:T(8,128)(2,1)S(1)}, u32[]{:S(2)}, u32[]{:S(2)}) collective-permute-start(bf16[2,4,64,192]{3,2,1,0:T(8,128)(2,1)S(1)} %fusion.21), channel_id=1, source_target_pairs={{0,2},{1,3},{4,6},{5,7},{8,10},{9,11},{12,14},{13,15},{16,18},{17,... | collective-permute-start | bytes 589832 | tf_op jit(solution)/shard_map/ppermute | solution.py:13
  7.2 5.5 %collective-permute-done = bf16[2,4,64,192]{3,2,1,0:T(8,128)(2,1)S(1)} collective-permute-done((bf16[2,4,64,192]{3,2,1,0:T(8,128)(2,1)S(1)}, bf16[2,4,64,192]{3,2,1,0:T(8,128)(2,1)S(1)}, u32[]{:S(2)}, u32[]{:S(2)}) %collective-permute-start) | collective-permute-done | bytes 196640 | tf_op jit(solution)/shard_map/ppermute | solution.py:13
  12.7 1.0 %broadcast_select_fusion = bf16[2,4,64,192]{3,2,1,0:T(8,128)(2,1)S(1)} fusion(bf16[2,4,64,192]{3,2,1,0:T(8,128)(2,1)} %param.8, bf16[2,4,64,192]{3,2,1,0:T(8,128)(2,1)S(1)} %collective-permute-done, pred[]{:T(512)S(6)} %eq.3), kind=kLoop, calls=%fused_computation.83 | loop fusion | flops 98304 | bytes 589825 | tf_op jit(solution)/shard_map/jit(_where)/select_n | solution.py:92
  13.8 3.5 %collective-permute-start.1 = (bf16[4,1,64,192]{3,2,1,0:T(8,128)(2,1)S(1)}, bf16[4,1,64,192]{3,2,1,0:T(8,128)(2,1)S(1)}, u32[]{:S(2)}, u32[]{:S(2)}) collective-permute-start(bf16[4,1,64,192]{3,2,1,0:T(8,128)(2,1)S(1)} %get-tuple-element.35), channel_id=1, source_target_pairs={{0,4},{4,8},{8,12},{1,5},{5,9},{9,13},{2,6},{6,10},{10,14},{3,7},{... | collective-permute-start | bytes 294920 | tf_op jit(solution)/shard_map/ppermute | solution.py:24
  17.3 1.3 %collective-permute-start.2 = (bf16[4,1,64,192]{3,2,1,0:T(8,128)(2,1)S(1)}, bf16[4,1,64,192]{3,2,1,0:T(8,128)(2,1)S(1)}, u32[]{:S(2)}, u32[]{:S(2)}) collective-permute-start(bf16[4,1,64,192]{3,2,1,0:T(8,128)(2,1)S(1)} %get-tuple-element.36), channel_id=1, source_target_pairs={{4,0},{8,4},{12,8},{5,1},{9,5},{13,9},{6,2},{10,6},{14,10},{7,3},{... | collective-permute-start | bytes 294920 | tf_op jit(solution)/shard_map/ppermute | solution.py:26
  18.6 1.1 %collective-permute-done.1 = bf16[4,1,64,192]{3,2,1,0:T(8,128)(2,1)S(1)} collective-permute-done((bf16[4,1,64,192]{3,2,1,0:T(8,128)(2,1)S(1)}, bf16[4,1,64,192]{3,2,1,0:T(8,128)(2,1)S(1)}, u32[]{:S(2)}, u32[]{:S(2)}) %collective-permute-start.1) | collective-permute-done | bytes 98336 | tf_op jit(solution)/shard_map/ppermute | solution.py:24
  19.8 4.4 %collective-permute-done.2 = bf16[4,1,64,192]{3,2,1,0:T(8,128)(2,1)S(1)} collective-permute-done((bf16[4,1,64,192]{3,2,1,0:T(8,128)(2,1)S(1)}, bf16[4,1,64,192]{3,2,1,0:T(8,128)(2,1)S(1)}, u32[]{:S(2)}, u32[]{:S(2)}) %collective-permute-start.2) | collective-permute-done | bytes 98336 | tf_op jit(solution)/shard_map/ppermute | solution.py:26
  24.2 1.6 %collective-permute-start.3 = (bf16[4,6,1,192]{3,2,1,0:T(2,128)(2,1)S(1)}, bf16[4,6,1,192]{3,2,1,0:T(2,128)(2,1)S(1)}, u32[]{:S(2)}, u32[]{:S(2)}) collective-permute-start(bf16[4,6,1,192]{3,2,1,0:T(2,128)(2,1)S(1)} %get-tuple-element.25), channel_id=1, source_target_pairs={{0,1},{2,3},{4,5},{6,7},{8,9},{10,11},{12,13},{14,15},{16,17},{18,... | collective-permute-start | bytes 27656 | tf_op jit(solution)/shard_map/ppermute | solution.py:24
  25.8 1.3 %collective-permute-start.4 = (bf16[4,6,1,192]{3,2,1,0:T(2,128)(2,1)S(1)}, bf16[4,6,1,192]{3,2,1,0:T(2,128)(2,1)S(1)}, u32[]{:S(2)}, u32[]{:S(2)}) collective-permute-start(bf16[4,6,1,192]{3,2,1,0:T(2,128)(2,1)S(1)} %get-tuple-element.26), channel_id=1, source_target_pairs={{1,0},{3,2},{5,4},{7,6},{9,8},{11,10},{13,12},{15,14},{17,16},{19,... | collective-permute-start | bytes 27656 | tf_op jit(solution)/shard_map/ppermute | solution.py:26
  27.1 0.2 pad_maximum_fusion.1
  27.5 0.2 fusion.50
  27.8 1.1 %collective-permute-done.4 = bf16[4,6,1,192]{3,2,1,0:T(2,128)(2,1)S(1)} collective-permute-done((bf16[4,6,1,192]{3,2,1,0:T(2,128)(2,1)S(1)}, bf16[4,6,1,192]{3,2,1,0:T(2,128)(2,1)S(1)}, u32[]{:S(2)}, u32[]{:S(2)}) %collective-permute-start.4) | collective-permute-done | bytes 9248 | tf_op jit(solution)/shard_map/ppermute | solution.py:26
  28.8 0.4 maximum_maximum_fusion
  29.3 0.6 %fusion.225 = (bf16[2,4,64,192]{3,2,1,0:T(8,128)(2,1)S(1)}, bf16[2,4,64,192]{3,2,1,0:T(8,128)(2,1)S(1)}, bf16[2,4,64,192]{3,2,1,0:T(8,128)(2,1)S(1)}, bf16[2,4,6...) fusion(bf16[4,6,65,192]{3,2,1,0:T(8,128)(2,1)S(1)} %get-tuple-e, ...), kind=kLoop, calls=%fused_computation.297 | loop fusion | bytes 7077888 | tf_op jit(solution)/shard_map/slice | solution.py:45
  29.9 0.3 fusion.45
  30.2 0.3 convolution_add_fusion.24
  30.4 0.3 convolution_add_fusion.23
  30.7 0.3 convolution_add_fusion.22
  31.0 0.3 fusion
  31.2 0.3 convolution_add_fusion.20
  31.5 0.3 convolution_add_fusion.19
  31.7 0.2 convolution_add_fusion.18
  32.0 0.3 convolution_add_fusion.17
  32.3 0.3 convolution_add_fusion.16
  32.5 0.3 convolution_add_fusion.15
  32.8 0.3 convolution_add_fusion.14
  33.0 0.3 convolution_add_fusion.13
  33.3 0.3 convolution_add_fusion.12
  33.5 0.3 convolution_add_fusion.11
  33.8 0.3 convolution_add_fusion.10
  34.1 0.3 convolution_add_fusion.9
  34.3 0.3 convolution_add_fusion.8
  34.6 0.3 convolution_add_fusion.7
  34.8 0.3 convolution_add_fusion.6
  35.1 0.3 convolution_add_fusion.5
  35.4 0.3 convolution_add_fusion.4
  35.7 0.3 convolution_add_fusion.3
  35.9 0.3 convolution_add_fusion.2
  36.2 0.3 convolution_add_fusion.1
  36.4 0.3 convolution_add_fusion
  37.0 3.5 %collective-permute-start.5 = (bf16[2,1,64,192]{3,2,1,0:T(8,128)(2,1)S(1)}, bf16[2,1,64,192]{3,2,1,0:T(8,128)(2,1)S(1)}, u32[]{:S(2)}, u32[]{:S(2)}) collective-permute-start(bf16[2,1,64,192]{3,2,1,0:T(8,128)(2,1)S(1)} %get-tuple-element.49), channel_id=1, source_target_pairs={{0,4},{4,8},{8,12},{1,5},{5,9},{9,13},{2,6},{6,10},{10,14},{3,7},{... | collective-permute-start | bytes 147464 | tf_op jit(solution)/shard_map/ppermute | solution.py:24
  40.5 1.3 %collective-permute-start.6 = (bf16[2,1,64,192]{3,2,1,0:T(8,128)(2,1)S(1)}, bf16[2,1,64,192]{3,2,1,0:T(8,128)(2,1)S(1)}, u32[]{:S(2)}, u32[]{:S(2)}) collective-permute-start(bf16[2,1,64,192]{3,2,1,0:T(8,128)(2,1)S(1)} %get-tuple-element.50), channel_id=1, source_target_pairs={{4,0},{8,4},{12,8},{5,1},{9,5},{13,9},{6,2},{10,6},{14,10},{7,3},{... | collective-permute-start | bytes 147464 | tf_op jit(solution)/shard_map/ppermute | solution.py:26
  42.0 0.2 convolution_add_fusion.28
  42.4 4.3 %collective-permute-done.6 = bf16[2,1,64,192]{3,2,1,0:T(8,128)(2,1)S(1)} collective-permute-done((bf16[2,1,64,192]{3,2,1,0:T(8,128)(2,1)S(1)}, bf16[2,1,64,192]{3,2,1,0:T(8,128)(2,1)S(1)}, u32[]{:S(2)}, u32[]{:S(2)}) %collective-permute-start.6) | collective-permute-done | bytes 49184 | tf_op jit(solution)/shard_map/ppermute | solution.py:26
  47.2 1.3 %collective-permute-start.7 = (bf16[2,6,1,192]{3,2,1,0:T(2,128)(2,1)S(1)}, bf16[2,6,1,192]{3,2,1,0:T(2,128)(2,1)S(1)}, u32[]{:S(2)}, u32[]{:S(2)}) collective-permute-start(bf16[2,6,1,192]{3,2,1,0:T(2,128)(2,1)S(1)} %get-tuple-element.45), channel_id=1, source_target_pairs={{0,1},{2,3},{4,5},{6,7},{8,9},{10,11},{12,13},{14,15},{16,17},{18,... | collective-permute-start | bytes 13832 | tf_op jit(solution)/shard_map/ppermute | solution.py:24
  48.5 1.3 %collective-permute-start.8 = (bf16[2,6,1,192]{3,2,1,0:T(2,128)(2,1)S(1)}, bf16[2,6,1,192]{3,2,1,0:T(2,128)(2,1)S(1)}, u32[]{:S(2)}, u32[]{:S(2)}) collective-permute-start(bf16[2,6,1,192]{3,2,1,0:T(2,128)(2,1)S(1)} %get-tuple-element.46), channel_id=1, source_target_pairs={{1,0},{3,2},{5,4},{7,6},{9,8},{11,10},{13,12},{15,14},{17,16},{19,... | collective-permute-start | bytes 13832 | tf_op jit(solution)/shard_map/ppermute | solution.py:26
  50.3 1.3 %collective-permute-done.8 = bf16[2,6,1,192]{3,2,1,0:T(2,128)(2,1)S(1)} collective-permute-done((bf16[2,6,1,192]{3,2,1,0:T(2,128)(2,1)S(1)}, bf16[2,6,1,192]{3,2,1,0:T(2,128)(2,1)S(1)}, u32[]{:S(2)}, u32[]{:S(2)}) %collective-permute-start.8) | collective-permute-done | bytes 4640 | tf_op jit(solution)/shard_map/ppermute | solution.py:26
  52.1 0.9 %fusion.120 = f32[512,96]{0,1:T(8,128)} fusion(bf16[512,192]{1,0:T(8,128)(2,1)S(1)} %bitcast.285, bf16[3,3,192,96]{3,2,1,0:T(8,128)(2,1)S(1)} %copy-done), kind=kOutput, calls=%fused_computation.198 | convolution fusion | flops 19003392 | bytes 557056 | tf_op jit(solution)/shard_map/dot_general | solution.py:80
  53.3 0.2 fusion.9
  53.7 0.2 convolution_add_fusion.40
  54.0 0.2 fusion.10
  54.2 0.7 %copy.16 = bf16[512,96]{1,0:T(8,128)(2,1)} copy(bf16[512,96]{0,1:T(8,128)(2,1)S(1)} %fusion.10) | data formatting | bytes 196608 | tf_op jit(solution)/shard_map/convert_element_type | solution.py:81
  55.3 0.2 fusion.7
  55.5 0.2 convolution_add_fusion.37
  55.7 0.2 convolution_add_fusion.36
  56.2 0.2 fusion.11
  56.5 1.1 %convolution_add_fusion.33 = f32[512,96]{0,1:T(8,128)S(1)} fusion(f32[512,96]{0,1:T(8,128)} %fusion.120, bf16[512,192]{1,0:T(8,128)(2,1)S(1)} %bitcast.287, bf16[3,3,192,96]{3,2,1,0:T(8,128)(2,1)S(1)} %copy-done), kind=kOutput, calls=%fused_computation.39 | convolution fusion | flops 18997248 | bytes 753664 | tf_op jit(solution)/shard_map/dot_general | solution.py:79
  57.9 0.2 convolution_add_fusion.31
  58.4 0.2 fusion.12
  58.8 0.2 convolution_add_fusion.27
  59.4 0.2 fusion.13
  60.2 0.8 %copy.20 = bf16[2,4,2,64,192]{4,3,2,1,0:T(8,128)(2,1)} copy(bf16[2,4,2,64,192]{4,3,1,0,2:T(8,128)(2,1)S(1)} %pad_maximum_fusion.2) | data formatting | bytes 786432 | tf_op jit(solution)/shard_map/stack | solution.py:84
  (48 shorter events, 5.1 us)
Async XLA Ops:
  2.3 10.4 %collective-permute-start = (bf16[2,4,64,192]{3,2,1,0:T(8,128)(2,1)S(1)}, bf16[2,4,64,192]{3,2,1,0:T(8,128)(2,1)S(1)}, u32[]{:S(2)}, u32[]{:S(2)}) collective-permute-start(bf16[2,4,64,192]{3,2,1,0:T(8,128)(2,1)S(1)} %fusion.21), channel_id=1, source_target_pairs={{0,2},{1,3},{4,6},{5,7},{8,10},{9,11},{12,14},{13,15},{16,18},{17,... | collective-permute-start | bytes 589832 | tf_op jit(solution)/shard_map/ppermute | solution.py:13
  13.8 6.0 %collective-permute-start.1 = (bf16[4,1,64,192]{3,2,1,0:T(8,128)(2,1)S(1)}, bf16[4,1,64,192]{3,2,1,0:T(8,128)(2,1)S(1)}, u32[]{:S(2)}, u32[]{:S(2)}) collective-permute-start(bf16[4,1,64,192]{3,2,1,0:T(8,128)(2,1)S(1)} %get-tuple-element.35), channel_id=1, source_target_pairs={{0,4},{4,8},{8,12},{1,5},{5,9},{9,13},{2,6},{6,10},{10,14},{3,7},{... | collective-permute-start | bytes 294920 | tf_op jit(solution)/shard_map/ppermute | solution.py:24
  17.3 6.9 %collective-permute-start.2 = (bf16[4,1,64,192]{3,2,1,0:T(8,128)(2,1)S(1)}, bf16[4,1,64,192]{3,2,1,0:T(8,128)(2,1)S(1)}, u32[]{:S(2)}, u32[]{:S(2)}) collective-permute-start(bf16[4,1,64,192]{3,2,1,0:T(8,128)(2,1)S(1)} %get-tuple-element.36), channel_id=1, source_target_pairs={{4,0},{8,4},{12,8},{5,1},{9,5},{13,9},{6,2},{10,6},{14,10},{7,3},{... | collective-permute-start | bytes 294920 | tf_op jit(solution)/shard_map/ppermute | solution.py:26
  24.2 3.3 %copy-start.1 = (bf16[3,3,3,192,192]{4,3,2,1,0:T(8,128)(2,1)S(1)}, bf16[3,3,3,192,192]{4,3,2,1,0:T(8,128)(2,1)}, u32[]{:S(2)}) copy-start(bf16[3,3,3,192,192]{4,3,2,1,0:T(8,128)(2,1)} %param.10) | copy-start | bytes 5971972
  24.2 3.6 %collective-permute-start.3 = (bf16[4,6,1,192]{3,2,1,0:T(2,128)(2,1)S(1)}, bf16[4,6,1,192]{3,2,1,0:T(2,128)(2,1)S(1)}, u32[]{:S(2)}, u32[]{:S(2)}) collective-permute-start(bf16[4,6,1,192]{3,2,1,0:T(2,128)(2,1)S(1)} %get-tuple-element.25), channel_id=1, source_target_pairs={{0,1},{2,3},{4,5},{6,7},{8,9},{10,11},{12,13},{14,15},{16,17},{18,... | collective-permute-start | bytes 27656 | tf_op jit(solution)/shard_map/ppermute | solution.py:24
  25.8 3.1 %collective-permute-start.4 = (bf16[4,6,1,192]{3,2,1,0:T(2,128)(2,1)S(1)}, bf16[4,6,1,192]{3,2,1,0:T(2,128)(2,1)S(1)}, u32[]{:S(2)}, u32[]{:S(2)}) collective-permute-start(bf16[4,6,1,192]{3,2,1,0:T(2,128)(2,1)S(1)} %get-tuple-element.26), channel_id=1, source_target_pairs={{1,0},{3,2},{5,4},{7,6},{9,8},{11,10},{13,12},{15,14},{17,16},{19,... | collective-permute-start | bytes 27656 | tf_op jit(solution)/shard_map/ppermute | solution.py:26
  35.6 1.3 %copy-start.2 = (bf16[2,4,64,192]{3,2,1,0:T(8,128)(2,1)S(1)}, bf16[2,4,64,192]{3,2,1,0:T(8,128)(2,1)}, u32[]{:S(2)}) copy-start(bf16[2,4,64,192]{3,2,1,0:T(8,128)(2,1)} %param.7) | copy-start | bytes 589828
  35.6 1.3 %copy-start.5 = (f32[192]{0:T(256)S(1)}, f32[192]{0:T(256)}, u32[]{:S(2)}) copy-start(f32[192]{0:T(256)} %param.11) | copy-start | bytes 2308
  35.9 5.9 %copy-start = (bf16[3,3,192,96]{3,2,1,0:T(8,128)(2,1)S(1)}, bf16[3,3,192,96]{3,2,1,0:T(8,128)(2,1)}, u32[]{:S(2)}) copy-start(bf16[3,3,192,96]{3,2,1,0:T(8,128)(2,1)} %param.12) | copy-start | bytes 995332
  37.0 5.4 %collective-permute-start.5 = (bf16[2,1,64,192]{3,2,1,0:T(8,128)(2,1)S(1)}, bf16[2,1,64,192]{3,2,1,0:T(8,128)(2,1)S(1)}, u32[]{:S(2)}, u32[]{:S(2)}) collective-permute-start(bf16[2,1,64,192]{3,2,1,0:T(8,128)(2,1)S(1)} %get-tuple-element.49), channel_id=1, source_target_pairs={{0,4},{4,8},{8,12},{1,5},{5,9},{9,13},{2,6},{6,10},{10,14},{3,7},{... | collective-permute-start | bytes 147464 | tf_op jit(solution)/shard_map/ppermute | solution.py:24
  40.5 6.2 %collective-permute-start.6 = (bf16[2,1,64,192]{3,2,1,0:T(8,128)(2,1)S(1)}, bf16[2,1,64,192]{3,2,1,0:T(8,128)(2,1)S(1)}, u32[]{:S(2)}, u32[]{:S(2)}) collective-permute-start(bf16[2,1,64,192]{3,2,1,0:T(8,128)(2,1)S(1)} %get-tuple-element.50), channel_id=1, source_target_pairs={{4,0},{8,4},{12,8},{5,1},{9,5},{13,9},{6,2},{10,6},{14,10},{7,3},{... | collective-permute-start | bytes 147464 | tf_op jit(solution)/shard_map/ppermute | solution.py:26
  47.2 3.0 %collective-permute-start.7 = (bf16[2,6,1,192]{3,2,1,0:T(2,128)(2,1)S(1)}, bf16[2,6,1,192]{3,2,1,0:T(2,128)(2,1)S(1)}, u32[]{:S(2)}, u32[]{:S(2)}) collective-permute-start(bf16[2,6,1,192]{3,2,1,0:T(2,128)(2,1)S(1)} %get-tuple-element.45), channel_id=1, source_target_pairs={{0,1},{2,3},{4,5},{6,7},{8,9},{10,11},{12,13},{14,15},{16,17},{18,... | collective-permute-start | bytes 13832 | tf_op jit(solution)/shard_map/ppermute | solution.py:24
  48.5 3.1 %collective-permute-start.8 = (bf16[2,6,1,192]{3,2,1,0:T(2,128)(2,1)S(1)}, bf16[2,6,1,192]{3,2,1,0:T(2,128)(2,1)S(1)}, u32[]{:S(2)}, u32[]{:S(2)}) collective-permute-start(bf16[2,6,1,192]{3,2,1,0:T(2,128)(2,1)S(1)} %get-tuple-element.46), channel_id=1, source_target_pairs={{1,0},{3,2},{5,4},{7,6},{9,8},{11,10},{13,12},{15,14},{17,16},{19,... | collective-permute-start | bytes 13832 | tf_op jit(solution)/shard_map/ppermute | solution.py:26
  51.8 2.1 %copy-start.4 = (f32[96]{0:T(128)S(1)}, f32[96]{0:T(128)}, u32[]{:S(2)}) copy-start(f32[96]{0:T(128)} %param.13) | copy-start | bytes 1156
  57.9 1.9 %copy-start.3 = (bf16[512,96]{1,0:T(8,128)(2,1)S(1)}, bf16[512,96]{1,0:T(8,128)(2,1)}, u32[]{:S(2)}) copy-start(bf16[512,96]{1,0:T(8,128)(2,1)} %copy.16) | copy-start | bytes 294916
where the time goes:
time: 61.4 us; the launch traced here: 61 us
  starting transfers between devices  19.9 us (32%)
  waiting for transfers between devices  17.8 us (29%)
  matrix products  14.6 us (24%)
  other arithmetic  4.82 us (8%)
  local copies, waits for them, and re-layouts  3.2 us (5%)
  between operations  0.71 us (1%)
    ppermute x4, waiting for transfers between devices, padded_2(): lax.ppermute(head, axis, [((i + 1) % count, i) for i in range(ends)])  11 us
    ppermute x4, starting transfers between devices, padded_2(): lax.ppermute(tail, axis, [(i, (i + 1) % count) for i in range(ends)])  9.82 us
    dot_general x27, matrix products, causal_conv(): jnp.dot(window, weight[a, b, c], preferred_element_type=jnp.float32)  6.8 us
    ppermute x1, waiting for transfers between devices, shifted(): return lax.ppermute(shard, axis, pairs)  5.52 us
    ppermute x4, starting transfers between devices, padded_2(): lax.ppermute(head, axis, [((i + 1) % count, i) for i in range(ends)])  5.17 us
    ppermute x1, starting transfers between devices, shifted(): return lax.ppermute(shard, axis, pairs)  4.89 us
    dot_general x12, matrix products, upsample_conv(): total = total + jnp.dot(window, upper, preferred_element_type=jnp.float32)  3.59 us
    dot_general x12, matrix products, upsample_conv(): total = total + jnp.dot(window, lower, preferred_element_type=jnp.float32)  3.34 us
  transfers between devices with their start and end apart: 9, of which 7 were waited for; matrix products, arithmetic and copies ran while one was open for 3% of the time, Pallas kernels for 0%

commit v1 on v0

v1 whole, which is shorter than its diff:
```python
import functools

import jax
import jax.numpy as jnp
from jax import lax
from jax.experimental import pallas as pl
from jax.experimental.pallas import tpu as pltpu
from jax.sharding import PartitionSpec as P


EPS = 1e-06
HALO = 2
LANES = 128
BLOCK = 16
SUBLANES = 8
AXES = ("ha", "ta", "wa")


def ring(axis):
    count = lax.axis_size(axis)
    return [(i, (i + 1) % count) for i in range(count)]


def snake(towards, later):
    chips, steps, cores = (lax.axis_size(axis) for axis in AXES)
    pairs = []
    for h in range(chips):
        for t in range(steps):
            for w in range(cores):
                step, target, core = (t + later) % steps, h + towards[w], w
                if not 0 <= target < chips:
                    target, core = h, cores - 1 - w
                pairs.append(((h * steps + t) * cores + w, (target * steps + step) * cores + core))
    return pairs


def activate(values, gain):
    wide = values.astype(jnp.float32)
    scale = lax.rsqrt(jnp.sum(wide * wide, axis=-1, keepdims=True) / wide.shape[-1] + EPS)
    v = wide * scale * gain
    return v / (1.0 + jnp.exp(-v))


def packed(cells):
    rest = jnp.concatenate([cells[0, :, :, LANES:], cells[1, :, :, LANES:]], axis=-1)
    return jnp.stack([cells[0, :, :, :LANES], cells[1, :, :, :LANES], rest])


def fetch(sources, targets, arrived):
    copies = [pltpu.make_async_copy(*pair, arrived.at[i]) for i, pair in enumerate(zip(sources, targets))]
    for copy in copies:
        copy.start()
    return copies


def pack_kernel(frames_hbm, cache_hbm, gain_hbm, first, second, raw_first, raw_second, act,
                frames, cache, gain, arrived):
    left = lax.axis_index("wa") == 0
    last = lax.axis_index("ta") == lax.axis_size("ta") - 1
    for copy in fetch((gain_hbm, frames_hbm, cache_hbm), (gain, frames, cache), arrived):
        copy.wait()
    cells = frames[...]
    active = activate(cells, gain[...].reshape(1, -1)).astype(jnp.bfloat16)
    act[...] = active
    sent = packed(jnp.where(last, cache[...], active))
    first[...] = jnp.where(left, sent[:, :HALO], sent[:, HALO:])
    second[...] = jnp.where(left, sent[:, HALO:], sent[:, :HALO])
    sent = packed(cells)
    raw_first[...] = jnp.where(left, sent[:, HALO:], sent[:, :HALO])
    raw_second[...] = jnp.where(left, sent[:, :HALO], sent[:, HALO:])


def prep_kernel(conv_hbm, up_hbm, gain_hbm, bias_hbm, up_bias_hbm, conv, folded, lines,
                weight, gain, bias, up_bias, arrived):
    copies = fetch((gain_hbm, bias_hbm, up_bias_hbm, up_hbm, conv_hbm), (gain, bias, up_bias, weight, conv), arrived)
    for copy in copies[:-1]:
        copy.wait()
    taps = [[weight[a, b].astype(jnp.float32) for b in range(3)] for a in range(3)]
    columns = []
    for rows in ((0,), (1, 2), (0, 1), (2,)):
        columns.append([functools.reduce(jnp.add, [taps[a][b] for a in rows]) for b in range(3)])
    for i, (one, two, three) in enumerate(columns):
        folded[2 * i] = jnp.concatenate([two + three, one + two], axis=-1).astype(jnp.bfloat16)
        folded[2 * i + 1] = jnp.concatenate([one, three], axis=-1).astype(jnp.bfloat16)
    line = up_bias[...].reshape(1, -1)
    for i, value in enumerate((gain[...].reshape(1, -1), bias[...].reshape(1, -1), jnp.concatenate([line, line], axis=-1))):
        lines[i] = jnp.broadcast_to(value, lines.shape[1:])
    copies[-1].wait()


def unpack(planes, cells, start):
    rows = planes.shape[1]
    rest = cells.shape[-1] - LANES
    for f in range(2):
        cells[f, pl.ds(start, rows), :, :LANES] = planes[f, :, :, :]
        cells[f, pl.ds(start, rows), :, LANES:] = planes[2, :, :, f * rest : (f + 1) * rest]


def edge_columns(near, edges, left):
    frames, rows = near.shape[0], near.shape[1]
    for f in range(frames):
        for r in range(rows):
            block = near[f, r].astype(jnp.float32)
            for s in range(HALO):
                line = jnp.where(left, block[s : s + 1], block[BLOCK - 1 - s : BLOCK - s])
                edges[f, s * rows + r : s * rows + r + 1, :] = line
        edges[f, HALO * rows :, :] = jnp.zeros((SUBLANES, near.shape[-1]), jnp.float32)


def conv_sums(cells, edges, weight, taps, rows):
    channels = cells.shape[-1]
    cols = cells.shape[2]
    sums = [None, None, None]
    for a, f in taps:
        for b in range(3):
            side = jnp.concatenate(
                [edges[f, b : b + SUBLANES], edges[f, SUBLANES + b : 2 * SUBLANES + b]], axis=0
            ).astype(jnp.bfloat16)
            window = jnp.concatenate(
                [cells[f, b : b + rows].reshape(rows * cols, channels), side], axis=0
            )
            for c in range(3):
                part = jnp.dot(window, weight[a, b, c], preferred_element_type=jnp.float32)
                sums[c] = part if sums[c] is None else sums[c] + part
    return sums


def shifted_sum(sums, before, after, rows, cols, left):
    channels = sums[0].shape[-1]
    size = rows * cols
    lo, hi = SUBLANES, SUBLANES + cols
    side = [total[size:] for total in sums]
    before[:, lo:hi, :] = sums[0][:size].reshape(rows, cols, channels)
    after[:, lo:hi, :] = sums[2][:size].reshape(rows, cols, channels)
    zero = jnp.zeros((1, channels), jnp.float32)
    for r in range(rows):
        before[r, lo - 1 : lo, :] = jnp.where(left, zero, side[0][r : r + 1])
        after[r, hi : hi + 1, :] = jnp.where(left, side[2][r : r + 1], zero)
    body = sums[1][:size].reshape(rows, cols, channels)
    body = body + before[:, lo - 1 : hi - 1, :] + after[:, lo + 1 : hi + 1, :]
    pad = jnp.zeros((SUBLANES - rows, channels), jnp.float32)
    inner = [jnp.concatenate([before[r, hi - 1 : hi, :] for r in range(rows)] + [pad], axis=0),
             jnp.concatenate([after[r, lo : lo + 1, :] for r in range(rows)] + [pad], axis=0)]
    outer = [side[0][SUBLANES:], side[2][SUBLANES:]]
    edge = side[1][:SUBLANES] + jnp.where(left, inner[0] + outer[1], outer[0] + inner[1])
    return body, edge


def place():
    chip = lax.axis_index("ha")
    core = lax.axis_index("wa")
    return core == 0, core, chip == 0, chip == lax.axis_size("ha") - 1


def row_valid(count, top, bottom, halo):
    row = lax.broadcasted_iota(jnp.int32, (count, 1), 0) % SUBLANES
    rows = SUBLANES if halo == HALO else SUBLANES - 2 * (HALO - halo)
    outside = (top & (row < halo)) | (bottom & (row >= rows - halo))
    return jnp.logical_not(outside)


def own_kernel(frames_hbm, act, top_a, top_b, sib, sib_ends, weight, lines, body_out, edge_out,
               frames, raw, cells, near, edges, live, before, after, arrived):
    copies = fetch((frames_hbm,), (frames,), arrived)
    left, core, top, bottom = place()
    count, rows, cols, channels = frames.shape
    gains, biases = lines[0, :1], lines[1, :1]
    far = rows + HALO
    upper, lower = core * far, (1 - core) * far
    unpack(top_a, raw, upper)
    unpack(top_b, raw, lower)
    cells[:, HALO:far] = act[...]
    for start, outside in ((0, top), (far, bottom)):
        value = activate(raw[:, start : start + HALO], gains).astype(jnp.bfloat16)
        cells[:, start : start + HALO] = jnp.where(outside, jnp.zeros_like(value), value)
    offset = pl.multiple_of(core * (cols - BLOCK), BLOCK)
    near[:, HALO:far] = sib[:, :, pl.ds(offset, BLOCK), :]
    unpack(sib_ends[:, :HALO], near, lower)
    unpack(sib_ends[:, HALO:], near, upper)
    edge_columns(near, edges, left)
    inside = row_valid(2 * SUBLANES, top, bottom, HALO)
    for f in range(count):
        value = activate(edges[f, : 2 * SUBLANES], gains)
        live[f, : 2 * SUBLANES] = jnp.where(inside, value, jnp.zeros_like(value))
        live[f, 2 * SUBLANES :] = jnp.zeros((SUBLANES, channels), jnp.float32)
    mid = rows + 2
    copies[0].wait()
    raw[:, HALO:far] = frames[...]
    for t in range(count):
        taps = [(a, t + a - 2) for a in range(3) if 0 <= t + a - 2]
        sums = conv_sums(cells, live, weight, taps, mid)
        body, edge = shifted_sum(sums, before, after, mid, cols, left)
        body_out[t] = body + raw[t, 1 : 1 + mid].astype(jnp.float32) + biases
        edge_out[t] = edge + edges[t, 1 : 1 + SUBLANES] + biases


def rest_kernel(main_a, main_b, top_a, top_b, sib, weight, body_in, edge_in, folded, lines, out,
                cells, near, edges, before, after, res, rim, wide):
    left, core, top, bottom = place()
    count, mid, cols, channels = body_in.shape
    rows = mid - 2
    far = rows + HALO
    unpack(main_a, cells, HALO + core * HALO)
    unpack(main_b, cells, HALO + (1 - core) * HALO)
    unpack(top_a, cells, core * far)
    unpack(top_b, cells, (1 - core) * far)
    zero = jnp.zeros((2, HALO, cols, channels), jnp.bfloat16)
    cells[:, :HALO] = jnp.where(top, zero, cells[:, :HALO])
    cells[:, far:] = jnp.where(bottom, zero, cells[:, far:])
    starts = (HALO + (1 - core) * HALO, HALO + core * HALO, (1 - core) * far, core * far)
    for i, start in enumerate(starts):
        unpack(sib[:, i * HALO : (i + 1) * HALO], near, start)
    edge_columns(near, edges, left)
    inside = row_valid(2 * SUBLANES, top, bottom, HALO)
    for f in range(2):
        value = edges[f, : 2 * SUBLANES]
        edges[f, : 2 * SUBLANES] = jnp.where(inside, value, jnp.zeros_like(value))
    ring_inside = row_valid(SUBLANES, top, bottom, 1)
    line = jnp.zeros((cols, channels), jnp.bfloat16)
    for t in range(count):
        taps = [(a, t + a) for a in range(3) if t + a < 2]
        if taps:
            sums = conv_sums(cells, edges, weight, taps, mid)
            body, edge = shifted_sum(sums, before, after, mid, cols, left)
            body, edge = body + body_in[t], edge + edge_in[t]
        else:
            body, edge = body_in[t], edge_in[t]
        body = body.astype(jnp.bfloat16)
        res[t] = body
        res[t, 0] = jnp.where(top, line, body[0])
        res[t, mid - 1] = jnp.where(bottom, line, body[mid - 1])
        rim[t, :SUBLANES] = jnp.where(ring_inside, edge, jnp.zeros_like(edge))
        rim[t, SUBLANES:] = jnp.zeros((SUBLANES, channels), jnp.float32)
    size = count * rows * cols
    lo, hi = SUBLANES, SUBLANES + cols
    lane = lax.broadcasted_iota(jnp.int32, (1, 1, channels), 2)
    early = lane < channels // 2
    nothing = jnp.zeros((1, channels), jnp.float32)
    windows = []
    for k in range(3):
        window = [res[t, k : k + rows].reshape(rows * cols, channels) for t in range(count)]
        window += [
            jnp.concatenate([rim[t, k : k + SUBLANES] for t in range(count)], axis=0).astype(jnp.bfloat16)
        ]
        windows.append(jnp.concatenate(window, axis=0))
    for p in range(2):
        centre = sides = None
        for k in range(2):
            i = 2 * (2 * p + k)
            one = jnp.dot(windows[p + k], folded[i], preferred_element_type=jnp.float32)
            two = jnp.dot(windows[p + k], folded[i + 1], preferred_element_type=jnp.float32)
            centre = one if centre is None else centre + one
            sides = two if sides is None else sides + two
        wide[:, lo:hi, :] = sides[:size].reshape(count * rows, cols, channels)
        for t in range(count):
            for r in range(rows):
                value = sides[size + t * SUBLANES + r : size + t * SUBLANES + r + 1]
                wide[t * rows + r, lo - 1 : lo, :] = jnp.where(left, nothing, value)
                wide[t * rows + r, hi : hi + 1, :] = jnp.where(left, value, nothing)
        total = centre[:size].reshape(count * rows, cols, channels)
        total = total + jnp.where(early, wide[:, lo - 1 : hi - 1, :], wide[:, lo + 1 : hi + 1, :])
        total = (total + lines[2, :1].reshape(1, 1, -1)).astype(jnp.bfloat16)
        for t in range(count):
            for r in range(rows):
                out[t, 2 * r + p] = total[t * rows + r]


VMEM = pl.BlockSpec(memory_space=pltpu.VMEM)
HBM = pl.BlockSpec(memory_space=pltpu.HBM)


def call(kernel, specs, shapes, scratch, flops, *args):
    return pl.pallas_call(
        kernel,
        out_shape=shapes,
        in_specs=specs,
        out_specs=jax.tree.map(lambda _: VMEM, shapes),
        scratch_shapes=scratch,
        cost_estimate=pl.CostEstimate(flops=flops, transcendentals=0, bytes_accessed=0),
        compiler_params=pltpu.CompilerParams(vmem_limit_bytes=40 * 1024 * 1024),
    )(*[pltpu.with_memory_space_constraint(arg, pltpu.HBM) if spec is HBM else arg for spec, arg in zip(specs, args)])


def near_sibling(parts):
    start = (1 - lax.axis_index("wa")) * (parts[0].shape[2] - BLOCK)
    return jnp.concatenate([lax.dynamic_slice_in_dim(part, start, BLOCK, axis=2) for part in parts], axis=1)


def block(frames, cache, norm_gain, conv_weight, conv_bias, up_weight, up_bias):
    count, rows, cols, channels = frames.shape
    outputs = up_weight.shape[-1]
    cores = lax.axis_size("wa")
    f32, bf16 = jnp.float32, jnp.bfloat16
    shape = jax.ShapeDtypeStruct
    part = shape((3, HALO, cols, LANES), bf16)
    sibling = [(i, cores - 1 - i) for i in range(cores)]
    along, against, later = snake((1, -1), 0), snake((-1, 1), 0), snake((1, -1), 1)
    sib = lax.ppermute(frames, "wa", sibling)
    first, second, raw_first, raw_second, act = call(
        pack_kernel, [HBM] * 3, (part, part, part, part, shape(frames.shape, bf16)),
        (pltpu.VMEM(frames.shape, bf16), pltpu.VMEM(cache.shape, bf16), pltpu.VMEM(norm_gain.shape, f32),
         pltpu.SemaphoreType.DMA((3,))),
        0, frames, cache, norm_gain,
    )
    main_a = lax.ppermute(first, "ta", ring("ta"))
    main_b = lax.ppermute(second, "ta", ring("ta"))
    prev_a = lax.ppermute(second, AXES, later)
    own_a = lax.ppermute(raw_first, AXES, along)
    own_b = lax.ppermute(raw_second, AXES, against)
    prev_b = lax.ppermute(main_a, AXES, against)
    sib_own = lax.ppermute(near_sibling([own_a, own_b]), "wa", sibling)
    sib_prev = lax.ppermute(near_sibling([main_a, main_b, prev_a, prev_b]), "wa", sibling)
    weight, folded, lines = call(
        prep_kernel, [HBM] * 5,
        (shape(conv_weight.shape, bf16), shape((8, channels, 2 * outputs), bf16), shape((3, SUBLANES, channels), f32)),
        (pltpu.VMEM(up_weight.shape, bf16), pltpu.VMEM(norm_gain.shape, f32), pltpu.VMEM(conv_bias.shape, f32),
         pltpu.VMEM(up_bias.shape, f32), pltpu.SemaphoreType.DMA((5,))),
        10**9, conv_weight, up_weight, norm_gain, conv_bias, up_bias,
    )
    mid, all_rows = rows + 2, rows + 2 * HALO
    grid = pltpu.VMEM((count, all_rows, cols, channels), bf16)
    near = pltpu.VMEM((count, all_rows, BLOCK, channels), bf16)
    edges = pltpu.VMEM((count, 3 * SUBLANES, channels), f32)
    shift = pltpu.VMEM((mid, cols + 2 * SUBLANES, channels), f32)
    body, edge = call(
        own_kernel, [HBM] + [VMEM] * 7,
        (shape((count, mid, cols, channels), f32), shape((count, SUBLANES, channels), f32)),
        (pltpu.VMEM(frames.shape, bf16), grid, grid, near, edges, edges, shift, shift, pltpu.SemaphoreType.DMA((1,))),
        10**9, frames, act, own_a, own_b, sib, sib_own, weight, lines,
    )
    return call(
        rest_kernel, [VMEM] * 10, shape((count, 2 * rows, cols, 2 * outputs), bf16),
        (grid, near, edges, shift, shift,
         pltpu.VMEM((count, mid, cols, channels), bf16), pltpu.VMEM((count, 2 * SUBLANES, channels), f32),
         pltpu.VMEM((count * rows, cols + 2 * SUBLANES, channels), f32)), 10**9,
        main_a, main_b, prev_a, prev_b, sib_prev, weight, body, edge, folded, lines,
    )


def solution(mesh):
    return jax.shard_map(
        block,
        mesh=mesh,
        in_specs=(
            P(("clips", "ta"), "ha", "wa", None),
            P("clips", "ha", "wa", None),
            P(),
            P(),
            P(),
            P(),
            P(),
        ),
        out_specs=P(("clips", "ta"), "ha", "wa", None),
        check_vma=False,
    )
```

time: 61.4 us -> 27.7 us (0.45)
  matrix products: 14.6 us -> 0 us
  starting transfers between devices: 19.9 us -> 8.18 us
  Pallas kernels: 0 us -> 9.79 us
  waiting for transfers between devices: 17.8 us -> 9.37 us
  other arithmetic: 4.82 us -> 0.02 us
  local copies, waits for them, and re-layouts: 3.2 us -> 0.04 us
    dot_general x55 -> x0, matrix products: 14.6 us -> none  [the longest x27 6.8 us: causal_conv(): jnp.dot(window, weight[a, b, c], preferred_element_type=jnp.float32)]
    ppermute x9, starting transfers between devices: 19.9 us -> 8.18 us  [the longest x1 3.07 us: block(): own_a = lax.ppermute(raw_first, AXES, along)]
    pallas_call x0 -> x4, Pallas kernels: none -> 9.79 us  [call(): pl.pallas_call(kernel, out_shape=shapes, in_specs=specs, out_specs=jax.tr...]
    ppermute x9, waiting for transfers between devices: 17.8 us -> 9.37 us  [the longest x1 4.69 us: block(): prev_b = lax.ppermute(main_a, AXES, against)]
    convert_element_type x2 -> x0, other arithmetic: 1.25 us -> none  [the longest x1 1.18 us: activate(): return jax.nn.silu(wide * scale * gain).astype(jnp.bfloat16)]
    convert_element_type x4 -> x0, local copies, waits for them, and re-layouts: 1.1 us -> none  [upsample_conv(): result = (total + bias).astype(jnp.bfloat16)]
    reduce_sum x1 -> x0, other arithmetic: 1.1 us -> none  [activate(): scale = lax.rsqrt(jnp.mean(wide * wide, axis=-1, keepdims=True) + EPS)]
    slice x5 -> x0, local copies, waits for them, and re-layouts: 1.04 us -> none  [the longest x2 0.83 us: causal_conv(): window = padded[a:a + count, b:b + rows, c:c + cols].reshape(-1, channels)]
  transfers between devices with their start and end apart: 9 -> 9, of which waited for: 7 -> 3; matrix products, arithmetic and copies ran while one was open for 3% -> 0% of each run, Pallas kernels for 0% -> 17%
where the time goes in v1:
time: 27.7 us; the launch traced here: 27.5 us
  Pallas kernels  9.79 us (35%)
  waiting for transfers between devices  9.37 us (34%)
  starting transfers between devices  8.18 us (30%)
    pallas_call x4, Pallas kernels, call(): pl.pallas_call(kernel, out_shape=shapes, in_specs=specs, out_specs=jax.tr...  9.79 us
    ppermute x1, waiting for transfers between devices, block(): prev_b = lax.ppermute(main_a, AXES, against)  4.69 us
    ppermute x1, waiting for transfers between devices, block(): own_b = lax.ppermute(raw_second, AXES, against)  4.61 us
    ppermute x1, starting transfers between devices, block(): own_a = lax.ppermute(raw_first, AXES, along)  3.07 us
    ppermute x1, starting transfers between devices, block(): prev_a = lax.ppermute(second, AXES, later)  2.5 us
    ppermute x1, starting transfers between devices, block(): main_a = lax.ppermute(first, 'ta', ring('ta'))  1.49 us
  transfers between devices with their start and end apart: 9, of which 3 were waited for; matrix products, arithmetic and copies ran while one was open for 0% of the time, Pallas kernels for 17%

profile of v1, /device:TPU:0, one launch (start us, length us, event | category | flops | bytes accessed | tf_op | source)
XLA Modules:
  0.0 27.5 jit_solution(465364686526700474)
XLA Ops:
  0.0 1.4 %shard_map.73 = (bf16[3,2,64,128]{3,2,1,0:T(8,128)(2,1)S(1)}, bf16[3,2,64,128]{3,2,1,0:T(8,128)(2,1)S(1)}, bf16[3,2,64,128]{3,2,1,0:T(8,128)(2,1)S(1)}, bf16[3,2...) custom-call(bf16[2,4,64,192]{3,2,1,0:T(8,128)(2,1)} %frames_hbm.3, bf16[2,4,64,192]{3,2,1,0:T(8,128)(2,1)} %cache_hbm.1, ...), custom_call_target="tpu_custom_call" | custom-call | tf_op jit(solution)/shard_map/pallas_call | solution.py:273
  1.4 3.1 %collective-permute-start.5 = (bf16[3,2,64,128]{3,2,1,0:T(8,128)(2,1)S(1)}, bf16[3,2,64,128]{3,2,1,0:T(8,128)(2,1)S(1)}, u32[]{:S(2)}, u32[]{:S(2)}) collective-permute-start(bf16[3,2,64,128]{3,2,1,0:T(8,128)(2,1)S(1)} %get-tuple-element.19), channel_id=1, source_target_pairs={{0,4},{1,0},{2,6},{3,2},{4,8},{5,1},{6,10},{7,3},{8,12},{9,5},{10,... | collective-permute-start | bytes 294920 | tf_op jit(solution)/shard_map/ppermute | solution.py:308
  4.5 0.0 collective-permute-start.7
  4.5 2.5 %collective-permute-start.2 = (bf16[3,2,64,128]{3,2,1,0:T(8,128)(2,1)S(1)}, bf16[3,2,64,128]{3,2,1,0:T(8,128)(2,1)S(1)}, u32[]{:S(2)}, u32[]{:S(2)}) collective-permute-start(bf16[3,2,64,128]{3,2,1,0:T(8,128)(2,1)S(1)} %get-tuple-element.16), channel_id=1, source_target_pairs={{0,6},{1,2},{2,4},{3,0},{4,10},{5,3},{6,8},{7,1},{8,14},{9,7},{10,... | collective-permute-start | bytes 294920 | tf_op jit(solution)/shard_map/ppermute | solution.py:307
  7.0 0.5 %collective-permute-start.1 = (bf16[3,2,64,128]{3,2,1,0:T(8,128)(2,1)S(1)}, bf16[3,2,64,128]{3,2,1,0:T(8,128)(2,1)S(1)}, u32[]{:S(2)}, u32[]{:S(2)}) collective-permute-start(bf16[3,2,64,128]{3,2,1,0:T(8,128)(2,1)S(1)} %get-tuple-element.16), channel_id=1, source_target_pairs={{0,2},{2,0},{1,3},{3,1},{4,6},{6,4},{5,7},{7,5},{8,10},{10,8},{9,1... | collective-permute-start | bytes 294920 | tf_op jit(solution)/shard_map/ppermute | solution.py:306
  7.5 1.5 %collective-permute-start = (bf16[3,2,64,128]{3,2,1,0:T(8,128)(2,1)S(1)}, bf16[3,2,64,128]{3,2,1,0:T(8,128)(2,1)S(1)}, u32[]{:S(2)}, u32[]{:S(2)}) collective-permute-start(bf16[3,2,64,128]{3,2,1,0:T(8,128)(2,1)S(1)} %get-tuple-element.15), channel_id=1, source_target_pairs={{0,2},{2,0},{1,3},{3,1},{4,6},{6,4},{5,7},{7,5},{8,10},{10,8},{9,1... | collective-permute-start | bytes 294920 | tf_op jit(solution)/shard_map/ppermute | solution.py:305
  9.0 0.0 collective-permute-done.5.top_a
  9.0 0.0 collective-permute-start.6
  9.0 4.6 %collective-permute-done.6.top_b = bf16[3,2,64,128]{3,2,1,0:T(8,128)(2,1)S(1)} collective-permute-done((bf16[3,2,64,128]{3,2,1,0:T(8,128)(2,1)S(1)}, bf16[3,2,64,128]{3,2,1,0:T(8,128)(2,1)S(1)}, u32[]{:S(2)}, u32[]{:S(2)}) %collective-permute-start.6) | collective-permute-done | bytes 98336 | tf_op jit(solution)/shard_map/ppermute | solution.py:309
  13.6 0.1 collective-permute-start.8
  13.7 0.1 collective-permute-done.main_a
  13.8 0.4 %collective-permute-start.3 = (bf16[3,2,64,128]{3,2,1,0:T(8,128)(2,1)S(1)}, bf16[3,2,64,128]{3,2,1,0:T(8,128)(2,1)S(1)}, u32[]{:S(2)}, u32[]{:S(2)}) collective-permute-start(bf16[3,2,64,128]{3,2,1,0:T(8,128)(2,1)S(1)} %collective-permute-done.main_a), channel_id=1, source_target_pairs={{0,1},{1,5},{2,3},{3,7},{4,0},{5,9},{6,2},{7,11},{8,4},{9,13},{10,... | collective-permute-start | bytes 294920 | tf_op jit(solution)/shard_map/ppermute | solution.py:310
  14.2 0.0 collective-permute-done.2.top_a
  14.2 0.0 collective-permute-done.1.main_b
  14.3 4.7 %collective-permute-done.3.top_b = bf16[3,2,64,128]{3,2,1,0:T(8,128)(2,1)S(1)} collective-permute-done((bf16[3,2,64,128]{3,2,1,0:T(8,128)(2,1)S(1)}, bf16[3,2,64,128]{3,2,1,0:T(8,128)(2,1)S(1)}, u32[]{:S(2)}, u32[]{:S(2)}) %collective-permute-start.3) | collective-permute-done | bytes 98336 | tf_op jit(solution)/shard_map/ppermute | solution.py:310
  19.0 0.1 collective-permute-start.4
  19.1 2.0 %shard_map.74 = (bf16[3,3,3,192,192]{4,3,2,1,0:T(8,128)(2,1)S(1)}, bf16[8,192,192]{2,1,0:T(8,128)(2,1)S(1)}, f32[3,8,192]{2,1,0:T(8,128)S(1)}) custom-call(bf16[3,3,3,192,192]{4,3,2,1,0:T(8,128)(2,1)} %conv_hbm.1, bf16[3,3,192,96]{3,2,1,0:T(8,128)(2,1)} %up_hbm.1, f32[192]{0:T(256)} %gain_hbm.3, f32[192]{0:T(256)} %bias_hbm.1, f32[96]{0:T(128)} %up_bias_hbm.1), custom_call_target="tpu_custom_call" | custom-call | flops 1000000000 | tf_op jit(solution)/shard_map/pallas_call | solution.py:273
  21.0 0.0 collective-permute-done.8.sib_ends
  21.1 0.0 collective-permute-done.7.sib
  21.1 2.8 %shard_map.75 = (f32[2,6,64,192]{3,2,1,0:T(8,128)S(1)}, f32[2,8,192]{2,1,0:T(8,128)S(1)}) custom-call(bf16[2,4,64,192]{3,2,1,0:T(8,128)(2,1)} %frames_hbm.3, bf16[2,4,64,192]{3,2,1,0:T(8,128)(2,1)S(1)} %get-tuple-element.18.act, bf16[3,2,64,128]{3,2,1,0:T(8,128)(2,1)S(1)} %collective-permute-done.5.top_a, ...), custom_call_target="tpu_custom_call" | custom-call | flops 1000000000 | tf_op jit(solution)/shard_map/pallas_call | solution.py:273
  23.8 0.0 collective-permute-done.4.sib
  23.8 3.7 %shard_map.76 = bf16[2,8,64,192]{3,2,1,0:T(8,128)(2,1)} custom-call(bf16[3,2,64,128]{3,2,1,0:T(8,128)(2,1)S(1)} %collective-permute-done.main_a, bf16[3,2,64,128]{3,2,1,0:T(8,128)(2,1)S(1)} %collective-permute-done.1.main_b, bf16[3,2,64,128]{3,2,1,0:T(8,128)(2,1)S(1)} %collective-permute-done.2.top_a, ...), custom_call_target="tpu_custom_call" | custom-call | flops 1000000000 | tf_op jit(solution)/shard_map/pallas_call | solution.py:273
  (8 shorter events, 0.1 us)
Async XLA Ops:
  1.4 7.6 %collective-permute-start.5 = (bf16[3,2,64,128]{3,2,1,0:T(8,128)(2,1)S(1)}, bf16[3,2,64,128]{3,2,1,0:T(8,128)(2,1)S(1)}, u32[]{:S(2)}, u32[]{:S(2)}) collective-permute-start(bf16[3,2,64,128]{3,2,1,0:T(8,128)(2,1)S(1)} %get-tuple-element.19), channel_id=1, source_target_pairs={{0,4},{1,0},{2,6},{3,2},{4,8},{5,1},{6,10},{7,3},{8,12},{9,5},{10,... | collective-permute-start | bytes 294920 | tf_op jit(solution)/shard_map/ppermute | solution.py:308
  4.5 16.6 %collective-permute-start.7 = (bf16[2,4,64,192]{3,2,1,0:T(8,128)(2,1)}, bf16[2,4,64,192]{3,2,1,0:T(8,128)(2,1)S(1)}, u32[]{:S(2)}, u32[]{:S(2)}) collective-permute-start(bf16[2,4,64,192]{3,2,1,0:T(8,128)(2,1)} %frames_hbm.3), channel_id=1, source_target_pairs={{0,1},{1,0},{2,3},{3,2},{4,5},{5,4},{6,7},{7,6},{8,9},{9,8},{10,11... | collective-permute-start | bytes 589832 | tf_op jit(solution)/shard_map/ppermute | solution.py:298
  4.5 9.8 %collective-permute-start.2 = (bf16[3,2,64,128]{3,2,1,0:T(8,128)(2,1)S(1)}, bf16[3,2,64,128]{3,2,1,0:T(8,128)(2,1)S(1)}, u32[]{:S(2)}, u32[]{:S(2)}) collective-permute-start(bf16[3,2,64,128]{3,2,1,0:T(8,128)(2,1)S(1)} %get-tuple-element.16), channel_id=1, source_target_pairs={{0,6},{1,2},{2,4},{3,0},{4,10},{5,3},{6,8},{7,1},{8,14},{9,7},{10,... | collective-permute-start | bytes 294920 | tf_op jit(solution)/shard_map/ppermute | solution.py:307
  7.0 7.3 %collective-permute-start.1 = (bf16[3,2,64,128]{3,2,1,0:T(8,128)(2,1)S(1)}, bf16[3,2,64,128]{3,2,1,0:T(8,128)(2,1)S(1)}, u32[]{:S(2)}, u32[]{:S(2)}) collective-permute-start(bf16[3,2,64,128]{3,2,1,0:T(8,128)(2,1)S(1)} %get-tuple-element.16), channel_id=1, source_target_pairs={{0,2},{2,0},{1,3},{3,1},{4,6},{6,4},{5,7},{7,5},{8,10},{10,8},{9,1... | collective-permute-start | bytes 294920 | tf_op jit(solution)/shard_map/ppermute | solution.py:306
  7.5 6.3 %collective-permute-start = (bf16[3,2,64,128]{3,2,1,0:T(8,128)(2,1)S(1)}, bf16[3,2,64,128]{3,2,1,0:T(8,128)(2,1)S(1)}, u32[]{:S(2)}, u32[]{:S(2)}) collective-permute-start(bf16[3,2,64,128]{3,2,1,0:T(8,128)(2,1)S(1)} %get-tuple-element.15), channel_id=1, source_target_pairs={{0,2},{2,0},{1,3},{3,1},{4,6},{6,4},{5,7},{7,5},{8,10},{10,8},{9,1... | collective-permute-start | bytes 294920 | tf_op jit(solution)/shard_map/ppermute | solution.py:305
  9.0 4.6 %collective-permute-start.6 = (bf16[3,2,64,128]{3,2,1,0:T(8,128)(2,1)S(1)}, bf16[3,2,64,128]{3,2,1,0:T(8,128)(2,1)S(1)}, u32[]{:S(2)}, u32[]{:S(2)}) collective-permute-start(bf16[3,2,64,128]{3,2,1,0:T(8,128)(2,1)S(1)} %get-tuple-element.20), channel_id=1, source_target_pairs={{0,1},{1,5},{2,3},{3,7},{4,0},{5,9},{6,2},{7,11},{8,4},{9,13},{10,... | collective-permute-start | bytes 294920 | tf_op jit(solution)/shard_map/ppermute | solution.py:309
  13.6 7.4 %collective-permute-start.8 = (bf16[3,4,16,128]{3,2,1,0:T(8,128)(2,1)S(1)}, bf16[3,4,16,128]{3,2,1,0:T(8,128)(2,1)S(1)}, u32[]{:S(2)}, u32[]{:S(2)}) collective-permute-start(bf16[3,4,16,128]{3,2,1,0:T(8,128)(2,1)S(1)} %pad_maximum_fusion.1), channel_id=1, source_target_pairs={{0,1},{1,0},{2,3},{3,2},{4,5},{5,4},{6,7},{7,6},{8,9},{9,8},{10,11... | collective-permute-start | bytes 147464 | tf_op jit(solution)/shard_map/ppermute | solution.py:311
  13.8 5.2 %collective-permute-start.3 = (bf16[3,2,64,128]{3,2,1,0:T(8,128)(2,1)S(1)}, bf16[3,2,64,128]{3,2,1,0:T(8,128)(2,1)S(1)}, u32[]{:S(2)}, u32[]{:S(2)}) collective-permute-start(bf16[3,2,64,128]{3,2,1,0:T(8,128)(2,1)S(1)} %collective-permute-done.main_a), channel_id=1, source_target_pairs={{0,1},{1,5},{2,3},{3,7},{4,0},{5,9},{6,2},{7,11},{8,4},{9,13},{10,... | collective-permute-start | bytes 294920 | tf_op jit(solution)/shard_map/ppermute | solution.py:310
  19.0 4.9 %collective-permute-start.4 = (bf16[3,8,16,128]{3,2,1,0:T(8,128)(2,1)S(1)}, bf16[3,8,16,128]{3,2,1,0:T(8,128)(2,1)S(1)}, u32[]{:S(2)}, u32[]{:S(2)}) collective-permute-start(bf16[3,8,16,128]{3,2,1,0:T(8,128)(2,1)S(1)} %pad_maximum_fusion), channel_id=1, source_target_pairs={{0,1},{1,0},{2,3},{3,2},{4,5},{5,4},{6,7},{7,6},{8,9},{9,8},{10,11... | collective-permute-start | bytes 294920 | tf_op jit(solution)/shard_map/ppermute | solution.py:312

commit v2 on v1

v2 whole, which is shorter than its diff:
```python
import functools

import jax
import jax.numpy as jnp
from jax import lax
from jax.experimental import pallas as pl
from jax.experimental.pallas import tpu as pltpu
from jax.sharding import PartitionSpec as P


EPS = 1e-06
HALO = 2
LANES = 128
COST = 10**9
BLOCK = 8
SUBLANES = 8
AXES = ("ha", "ta", "wa")


def ring(axis):
    count = lax.axis_size(axis)
    return [(i, (i + 1) % count) for i in range(count)]


def snake(towards, later):
    chips, steps, cores = (lax.axis_size(axis) for axis in AXES)
    pairs = []
    for h in range(chips):
        for t in range(steps):
            for w in range(cores):
                step, target, core = (t + later) % steps, h + towards[w], w
                if not 0 <= target < chips:
                    target, core = h, cores - 1 - w
                pairs.append(((h * steps + t) * cores + w, (target * steps + step) * cores + core))
    return pairs


def activate(values, gain):
    wide = values.astype(jnp.float32)
    scale = lax.rsqrt(jnp.sum(wide * wide, axis=-1, keepdims=True) / wide.shape[-1] + EPS)
    v = wide * scale * gain
    return v / (1.0 + jnp.exp(-v))


def packed(cells):
    rest = jnp.concatenate([cells[0, :, :, LANES:], cells[1, :, :, LANES:]], axis=-1)
    return jnp.stack([cells[0, :, :, :LANES], cells[1, :, :, :LANES], rest])


def fetch(sources, targets, arrived):
    copies = [pltpu.make_async_copy(*pair, arrived.at[i]) for i, pair in enumerate(zip(sources, targets))]
    for copy in copies:
        copy.start()
    return copies


def pack_kernel(frames_hbm, cache_hbm, gain_hbm, first, second, raw_first, raw_second, act,
                frames, cache, gain, arrived):
    left = lax.axis_index("wa") == 0
    last = lax.axis_index("ta") == lax.axis_size("ta") - 1
    copies = fetch((gain_hbm, frames_hbm, cache_hbm), (gain, frames, cache), arrived)
    for copy in copies[:2]:
        copy.wait()
    cells = frames[...]
    active = activate(cells, gain[...].reshape(1, -1)).astype(jnp.bfloat16)
    act[...] = active
    copies[2].wait()
    sent = packed(jnp.where(last, cache[...], active))
    first[...] = jnp.where(left, sent[:, :HALO], sent[:, HALO:])
    second[...] = jnp.where(left, sent[:, HALO:], sent[:, :HALO])
    sent = packed(cells)
    raw_first[...] = jnp.where(left, sent[:, HALO:], sent[:, :HALO])
    raw_second[...] = jnp.where(left, sent[:, :HALO], sent[:, HALO:])


def place():
    chip = lax.axis_index("ha")
    core = lax.axis_index("wa")
    return core == 0, core, chip == 0, chip == lax.axis_size("ha") - 1


def unpack(planes, cells, start):
    rows = planes.shape[1]
    rest = cells.shape[-1] - LANES
    for f in range(2):
        cells[f, pl.ds(start, rows), :, :LANES] = planes[f, :, :, :]
        cells[f, pl.ds(start, rows), :, LANES:] = planes[2, :, :, f * rest : (f + 1) * rest]


def clear_outside(cells, top, bottom):
    zero = jnp.zeros((2, HALO) + cells.shape[2:], cells.dtype)
    cells[:, :HALO] = jnp.where(top, zero, cells[:, :HALO])
    cells[:, HALO:] = jnp.where(bottom, zero, cells[:, HALO:])


def row_sums(inner, outer, weight, c, mid):
    parts = [[] for _ in range(mid)]
    for b in range(3):
        if inner:
            rows, cols, channels = inner[0][1].shape
            total = None
            for a, cells in inner:
                part = jnp.dot(cells.reshape(rows * cols, channels), weight[a, b, c], preferred_element_type=jnp.float32)
                total = part if total is None else total + part
            for r in range(rows):
                parts[r + HALO - b].append(total[r * cols : (r + 1) * cols])
        if outer:
            cols, channels = outer[0][1].shape[1:]
            total = None
            for a, cells in outer:
                window = cells[b : b + HALO].reshape(HALO * cols, channels)
                part = jnp.dot(window, weight[a, b, c], preferred_element_type=jnp.float32)
                total = part if total is None else total + part
            for r, target in enumerate(((0, 1), (0, mid - 1), (mid - 2, mid - 1))[b]):
                parts[target].append(total[r * cols : (r + 1) * cols])
    return [functools.reduce(jnp.add, part) if part else None for part in parts]


def add_taps(inner, outer, weight, base, rim, before, after, left):
    mid = len(base)
    channels = weight.shape[-1]
    lo, hi = SUBLANES, before.shape[1] - SUBLANES
    zero = jnp.zeros((1, channels), jnp.float32)
    first, second, third = [row_sums(inner, outer, weight, c, mid) for c in range(3)]
    total, line = [], []
    for r in range(mid):
        if second[r] is None:
            total.append(base[r])
            line.append(zero)
            continue
        before[r, lo - 1 : lo, :] = zero
        after[r, hi : hi + 1, :] = zero
        before[r, lo:hi, :] = first[r]
        after[r, lo:hi, :] = third[r]
        value = second[r] + before[r, lo - 1 : hi - 1, :] + after[r, lo + 1 : hi + 1, :]
        total.append(value if base[r] is None else base[r] + value)
        line.append(jnp.where(left, before[r, hi - 1 : hi, :], after[r, lo : lo + 1, :]))
    line = jnp.concatenate(line + [zero] * (SUBLANES - mid), axis=0)
    return total, line if rim is None else rim + line


def first_kernel(raw_first, raw_second, act, weight, bias, body_out, edge_out, frames, before, after):
    left, core, _, _ = place()
    count, mid, cols, channels = body_out.shape
    unpack(raw_first, frames, (1 - core) * HALO)
    unpack(raw_second, frames, core * HALO)
    line = bias[...].reshape(1, -1)
    none = jnp.broadcast_to(line, (cols, channels))
    for t in range(count):
        inner = [(a, act[t + a - 2]) for a in range(3) if 0 <= t + a - 2]
        base = [none] + [frames[t, r].astype(jnp.float32) + line for r in range(mid - 2)] + [none]
        total, edge = add_taps(inner, [], weight, base, None, before, after, left)
        for r in range(mid):
            body_out[t, r] = total[r]
        edge_out[t] = edge


def second_kernel(main_a, main_b, own_a, own_b, weight, gain, body_in, edge_in, body_out, edge_out,
                  main, raw, halo, before, after):
    left, core, top, bottom = place()
    count, mid, _, _ = body_in.shape
    unpack(main_a, main, core * HALO)
    unpack(main_b, main, (1 - core) * HALO)
    unpack(own_a, raw, core * HALO)
    unpack(own_b, raw, (1 - core) * HALO)
    halo[...] = activate(raw[...], gain[...].reshape(1, -1)).astype(jnp.bfloat16)
    clear_outside(halo, top, bottom)
    for t in range(count):
        inner = [(a, main[t + a]) for a in range(3) if t + a < 2]
        outer = [(a, halo.at[t + a - 2]) for a in range(3) if 0 <= t + a - 2]
        base = [body_in[t, r] for r in range(mid)]
        base[0] = base[0] + raw[t, HALO - 1].astype(jnp.float32)
        base[-1] = base[-1] + raw[t, HALO].astype(jnp.float32)
        total, edge = add_taps(inner, outer, weight, base, edge_in[t], before, after, left)
        for r in range(mid):
            body_out[t, r] = total[r]
        edge_out[t] = edge


def fold_kernel(weight, folded):
    taps = [[weight[a, b].astype(jnp.float32) for b in range(3)] for a in range(3)]
    columns = []
    for rows in ((0,), (1, 2), (0, 1), (2,)):
        columns.append([functools.reduce(jnp.add, [taps[a][b] for a in rows]) for b in range(3)])
    for i, (one, two, three) in enumerate(columns):
        folded[2 * i] = jnp.concatenate([two + three, one + two], axis=-1).astype(jnp.bfloat16)
        folded[2 * i + 1] = jnp.concatenate([one, three], axis=-1).astype(jnp.bfloat16)


def phase_sums(windows, folded, p):
    centre = sides = None
    for k in range(2):
        i = 2 * (2 * p + k)
        one = jnp.dot(windows[p + k], folded[i], preferred_element_type=jnp.float32)
        two = jnp.dot(windows[p + k], folded[i + 1], preferred_element_type=jnp.float32)
        centre = one if centre is None else centre + one
        sides = two if sides is None else sides + two
    return centre, sides


def phase_lines(bias, channels):
    line = bias[...].reshape(1, -1)
    early = lax.broadcasted_iota(jnp.int32, (1, channels), 1) < channels // 2
    return jnp.concatenate([line, line], axis=-1), early


def third_kernel(prev_a, prev_b, weight, folded, up_bias, body_in, edge_in, block_out, edge_out, out,
                 halo, before, after, res, wide):
    left, core, top, bottom = place()
    count, mid, cols, channels = body_in.shape
    unpack(prev_a, halo, core * HALO)
    unpack(prev_b, halo, (1 - core) * HALO)
    clear_outside(halo, top, bottom)
    for t in range(count):
        outer = [(a, halo.at[t + a]) for a in range(3) if t + a < 2]
        base = [body_in[t, r] for r in range(mid)]
        total, line = add_taps([], outer, weight, base, edge_in[t], before, after, left)
        edge_out[t] = line
        for r in range(mid):
            block_out[t, r] = jnp.where(left, total[r][cols - BLOCK :], total[r][:BLOCK])
            value = total[r].astype(jnp.bfloat16)
            if r in (0, mid - 1):
                value = jnp.where(bottom if r else top, jnp.zeros_like(value), value)
            res[t, r] = value
    rows = mid - 2
    lo, hi = SUBLANES, SUBLANES + cols
    line, early = phase_lines(up_bias, channels)
    nothing = jnp.zeros((1, channels), jnp.float32)
    for t in range(count):
        windows = [res[t, k : k + rows].reshape(rows * cols, channels) for k in range(3)]
        for p in range(2):
            centre, sides = phase_sums(windows, folded, p)
            for r in range(rows):
                wide[p, r, lo:hi, :] = sides[r * cols : (r + 1) * cols]
                wide[p, r, lo - 1 : lo, :] = nothing
                wide[p, r, hi : hi + 1, :] = nothing
                total = centre[r * cols : (r + 1) * cols]
                total = total + jnp.where(early, wide[p, r, lo - 1 : hi - 1, :], wide[p, r, lo + 1 : hi + 1, :])
                out[t, 2 * r + p] = (total + line).astype(jnp.bfloat16)


def edge_columns(near, edges, left):
    frames, rows = near.shape[0], near.shape[1]
    for f in range(frames):
        for r in range(rows):
            block = near[f, r].astype(jnp.float32)
            for s in range(HALO):
                line = jnp.where(left, block[s : s + 1], block[BLOCK - 1 - s : BLOCK - s])
                edges[f, s * rows + r : s * rows + r + 1, :] = line
        edges[f, HALO * rows :, :] = jnp.zeros((SUBLANES, near.shape[-1]), jnp.float32)


def near_kernel(*refs):
    left = lax.axis_index("wa") == 0
    out, start = refs[-1], 0
    for part in refs[:-1]:
        rows, cols = part.shape[1:3]
        out[:, start : start + rows] = jnp.where(left, part[:, :, cols - BLOCK :, :], part[:, :, :BLOCK, :])
        start += rows


def row_valid(count, rows, top, bottom, halo):
    row = lax.broadcasted_iota(jnp.int32, (count, 1), 0) % SUBLANES
    return jnp.logical_not((top & (row < halo)) | (bottom & (row >= rows - halo)))


def last_kernel(sib, weight, block_in, edge_in, folded, gain, bias, up_bias, done, out_hbm,
                near_prev, near_own, edges, raw, wide, block, sent):
    left, core, top, bottom = place()
    count, mid, _, channels = block_in.shape
    rows = mid - 2
    cols = done.shape[2]
    far = rows + HALO
    rest = pl.ds(pl.multiple_of(core * BLOCK, BLOCK), cols - BLOCK)
    strip = pl.ds(pl.multiple_of((1 - core) * (cols - BLOCK), BLOCK), BLOCK)
    copies = [
        pltpu.make_async_copy(done.at[t, :, rest, :], out_hbm.at[t, :, rest, :], sent.at[t]) for t in range(count)
    ]
    for copy in copies:
        copy.start()
    starts = (HALO + (1 - core) * HALO, HALO + core * HALO, (1 - core) * far, core * far)
    for i, start in enumerate(starts):
        unpack(sib[:, i * HALO : (i + 1) * HALO], near_prev, start)
    starts = ((1 - core) * far, core * far, HALO + core * HALO, HALO + (1 - core) * HALO)
    for i, start in enumerate(starts):
        unpack(sib[:, 4 * HALO + i * HALO : 4 * HALO + (i + 1) * HALO], near_own, start)
    edge_columns(near_prev, edges.at[:2], left)
    edge_columns(near_own, raw, left)
    inside = row_valid(2 * SUBLANES, SUBLANES, top, bottom, HALO)
    for f in range(2 + count):
        value = edges[f, : 2 * SUBLANES] if f < 2 else activate(raw[f - 2, : 2 * SUBLANES], gain[...].reshape(1, -1))
        edges[f, : 2 * SUBLANES] = jnp.where(inside, value, jnp.zeros_like(value))
        edges[f, 2 * SUBLANES :] = jnp.zeros((SUBLANES, channels), jnp.float32)
    sums = [None] * 3
    for b in range(3):
        side = [
            jnp.concatenate([edges[f, b : b + SUBLANES], edges[f, SUBLANES + b : 2 * SUBLANES + b]], axis=0)
            .astype(jnp.bfloat16)
            for f in range(2 + count)
        ]
        for a in range(3):
            window = jnp.concatenate(side[a : a + count], axis=0)
            for c in range(3):
                part = jnp.dot(window, weight[a, b, c], preferred_element_type=jnp.float32)
                sums[c] = part if sums[c] is None else sums[c] + part
    inside = row_valid(SUBLANES, mid, top, bottom, 1)
    row = lax.broadcasted_iota(jnp.int32, (SUBLANES, 1), 0)
    blank = jnp.zeros((SUBLANES, channels), jnp.float32)
    inner, rim = [], []
    for t in range(count):
        near = [total[2 * SUBLANES * t : 2 * SUBLANES * t + SUBLANES] for total in sums]
        next_ = [total[2 * SUBLANES * t + SUBLANES : 2 * SUBLANES * (t + 1)] for total in sums]
        edge = edge_in[t] + near[1] + jnp.where(left, next_[2], next_[0])
        edge = edge + raw[t, 1 : 1 + SUBLANES] + bias[...].reshape(1, -1)
        edges[t, :SUBLANES] = jnp.where(inside, edge, blank)
        rim.append(edges.at[t])
        lines = []
        for r in range(mid):
            change = jnp.where(left, near[2][r : r + 1], near[0][r : r + 1])
            value = block_in[t, r] + jnp.where(row == jnp.where(left, BLOCK - 1, 0), change, blank)
            if r in (0, mid - 1):
                value = jnp.where(bottom if r else top, blank, value)
            lines.append(value)
        inner.append(lines)
    windows = [
        jnp.concatenate(
            [value for lines in inner for value in lines[k : k + rows]] + [line[k : k + SUBLANES] for line in rim], axis=0
        ).astype(jnp.bfloat16)
        for k in range(3)
    ]
    line, early = phase_lines(up_bias, channels)
    nothing = jnp.zeros((1, channels), jnp.float32)
    fresh = (left & (row >= BLOCK - 2)) | (jnp.logical_not(left) & (row < 2))
    size = count * rows * BLOCK
    lo, hi = SUBLANES, SUBLANES + BLOCK
    for p in range(2):
        centre, sides = phase_sums(windows, folded, p)
        for t in range(count):
            for r in range(rows):
                at = t * rows + r
                value = sides[size + t * SUBLANES + r : size + t * SUBLANES + r + 1]
                wide[p, at, lo:hi, :] = sides[at * BLOCK : (at + 1) * BLOCK]
                wide[p, at, lo - 1 : lo, :] = jnp.where(left, nothing, value)
                wide[p, at, hi : hi + 1, :] = jnp.where(left, value, nothing)
                total = centre[at * BLOCK : (at + 1) * BLOCK] + line
                total = total + jnp.where(early, wide[p, at, lo - 1 : hi - 1, :], wide[p, at, lo + 1 : hi + 1, :])
                old = jnp.where(left, done[t, 2 * r + p, cols - BLOCK :, :], done[t, 2 * r + p, :BLOCK, :])
                block[t, 2 * r + p] = jnp.where(fresh, total, old.astype(jnp.float32)).astype(jnp.bfloat16)
    for t in range(count):
        copies.append(pltpu.make_async_copy(block.at[t], out_hbm.at[t, :, strip, :], sent.at[count + t]))
        copies[-1].start()
    for copy in copies:
        copy.wait()


VMEM = pl.BlockSpec(memory_space=pltpu.VMEM)
HBM = pl.BlockSpec(memory_space=pltpu.HBM)


def call(kernel, specs, shapes, scratch, flops, *args, outs=VMEM):
    return pl.pallas_call(
        kernel,
        out_shape=shapes,
        in_specs=specs,
        out_specs=jax.tree.map(lambda _: outs, shapes),
        scratch_shapes=scratch,
        cost_estimate=pl.CostEstimate(flops=flops, transcendentals=0, bytes_accessed=0),
        compiler_params=pltpu.CompilerParams(vmem_limit_bytes=16 * 1024 * 1024),
    )(*[pltpu.with_memory_space_constraint(arg, pltpu.HBM) if spec is HBM else arg for spec, arg in zip(specs, args)])


def block(frames, cache, norm_gain, conv_weight, conv_bias, up_weight, up_bias):
    count, rows, cols, channels = frames.shape
    outputs = up_weight.shape[-1]
    cores = lax.axis_size("wa")
    f32, bf16 = jnp.float32, jnp.bfloat16
    shape = jax.ShapeDtypeStruct
    part = shape((3, HALO, cols, LANES), bf16)
    sibling = [(i, cores - 1 - i) for i in range(cores)]
    along, against, later = snake((1, -1), 0), snake((-1, 1), 0), snake((1, -1), 1)
    first, second, raw_first, raw_second, act = call(
        pack_kernel, [HBM] * 3, (part, part, part, part, shape(frames.shape, bf16)),
        (pltpu.VMEM(frames.shape, bf16), pltpu.VMEM(cache.shape, bf16), pltpu.VMEM(norm_gain.shape, f32),
         pltpu.SemaphoreType.DMA((3,))),
        COST, frames, cache, norm_gain,
    )
    main_a = lax.ppermute(first, "ta", ring("ta"))
    main_b = lax.ppermute(second, "ta", ring("ta"))
    prev_a = lax.ppermute(second, AXES, later)
    own_a = lax.ppermute(raw_first, AXES, along)
    own_b = lax.ppermute(raw_second, AXES, against)
    prev_b = lax.ppermute(main_a, AXES, against)
    sib = call(
        near_kernel, [VMEM] * 8, shape((3, 4 * rows, BLOCK, LANES), bf16), (), 0,
        main_a, main_b, prev_a, prev_b, own_a, own_b, raw_first, raw_second,
    )
    sib = lax.ppermute(sib, "wa", sibling)
    mid, all_rows = rows + 2, rows + 2 * HALO
    body_shape = shape((count, mid, cols, channels), f32)
    edge_shape = shape((count, SUBLANES, channels), f32)
    shift = pltpu.VMEM((mid, cols + 2 * SUBLANES, channels), f32)
    tile = pltpu.VMEM((2, rows, cols, channels), bf16)
    halo = pltpu.VMEM((2, 2 * HALO, cols, channels), bf16)
    body, edge = call(
        first_kernel, [VMEM] * 5, (body_shape, edge_shape), (tile, shift, shift),
        10**9, raw_first, raw_second, act, conv_weight, conv_bias,
    )
    body, edge = call(
        second_kernel, [VMEM] * 8, (body_shape, edge_shape), (tile, halo, halo, shift, shift),
        10**9, main_a, main_b, own_a, own_b, conv_weight, norm_gain, body, edge,
    )
    folded = call(fold_kernel, [VMEM], shape((8, channels, 2 * outputs), bf16), (), 10**8, up_weight)
    out_shape = (count, 2 * rows, cols, 2 * outputs)
    block, edge, out = call(
        third_kernel, [VMEM] * 7,
        (shape((count, mid, BLOCK, channels), f32), edge_shape, shape(out_shape, bf16)),
        (halo, shift, shift, pltpu.VMEM((count, mid, cols, channels), bf16),
         pltpu.VMEM((2, rows, cols + 2 * SUBLANES, channels), f32)), 10**9,
        prev_a, prev_b, conv_weight, folded, up_bias, body, edge,
    )
    near = pltpu.VMEM((2, all_rows, BLOCK, channels), bf16)
    return call(
        last_kernel, [VMEM] * 9, shape(out_shape, bf16),
        (near, near, pltpu.VMEM((2 + count, 3 * SUBLANES, channels), f32), pltpu.VMEM((count, 3 * SUBLANES, channels), f32),
         pltpu.VMEM((2, count * rows, BLOCK + 2 * SUBLANES, channels), f32),
         pltpu.VMEM((count, 2 * rows, BLOCK, 2 * outputs), bf16), pltpu.SemaphoreType.DMA((2 * count,))),
        10**9, sib, conv_weight, block, edge, folded, norm_gain, conv_bias, up_bias, out, outs=HBM,
    )


def solution(mesh):
    return jax.shard_map(
        block,
        mesh=mesh,
        in_specs=(
            P(("clips", "ta"), "ha", "wa", None),
            P("clips", "ha", "wa", None),
            P(),
            P(),
            P(),
            P(),
            P(),
        ),
        out_specs=P(("clips", "ta"), "ha", "wa", None),
        check_vma=False,
    )
```

time: 27.7 us -> 20.5 us (0.74)
  waiting for transfers between devices: 9.37 us -> 4.23 us
  Pallas kernels: 9.79 us -> 8.27 us
  starting transfers between devices: 8.18 us -> 7.75 us
    ppermute x1, waiting for transfers between devices: 4.69 us -> 1.13 us  [block(): prev_b = lax.ppermute(main_a, AXES, against)]
    ppermute x1, waiting for transfers between devices: 4.61 us -> 2.03 us  [block(): own_b = lax.ppermute(raw_second, AXES, against)]
    ppermute x1, starting transfers between devices: 1.49 us -> 3.04 us  [block(): main_a = lax.ppermute(first, 'ta', ring('ta'))]
    pallas_call x4 -> x7, Pallas kernels: 9.79 us -> 8.27 us  [call(): pl.pallas_call(kernel, out_shape=shapes, in_specs=specs, out_specs=jax.tr...]
    ppermute x1, starting transfers between devices: 3.07 us -> 1.58 us  [block(): own_a = lax.ppermute(raw_first, AXES, along)]
    ppermute x1, waiting for transfers between devices: 0.01 us -> 1.06 us  [block(): main_b = lax.ppermute(second, 'ta', ring('ta'))]
    ppermute x1, starting transfers between devices: 0.54 us -> 1.49 us  [block(): main_b = lax.ppermute(second, 'ta', ring('ta'))]
    ppermute x1, starting transfers between devices: 2.5 us -> 1.55 us  [block(): prev_a = lax.ppermute(second, AXES, later)]
  transfers between devices with their start and end apart: 9 -> 7, of which waited for: 3 -> 3; matrix products, arithmetic and copies ran while one was open for 0% -> 0% of each run, Pallas kernels for 17% -> 24%
where the time goes in v2:
time: 20.5 us; the launch traced here: 20.4 us
  Pallas kernels  8.27 us (40%)
  starting transfers between devices  7.75 us (38%)
  waiting for transfers between devices  4.23 us (21%)
    pallas_call x7, Pallas kernels, call(): pl.pallas_call(kernel, out_shape=shapes, in_specs=specs, out_specs=jax.tr...  8.27 us
    ppermute x1, starting transfers between devices, block(): main_a = lax.ppermute(first, 'ta', ring('ta'))  3.04 us
    ppermute x1, waiting for transfers between devices, block(): own_b = lax.ppermute(raw_second, AXES, against)  2.03 us
    ppermute x1, starting transfers between devices, block(): own_a = lax.ppermute(raw_first, AXES, along)  1.58 us
    ppermute x1, starting transfers between devices, block(): prev_a = lax.ppermute(second, AXES, later)  1.55 us
    ppermute x1, starting transfers between devices, block(): main_b = lax.ppermute(second, 'ta', ring('ta'))  1.49 us
    ppermute x1, waiting for transfers between devices, block(): prev_b = lax.ppermute(main_a, AXES, against)  1.13 us
    ppermute x1, waiting for transfers between devices, block(): main_b = lax.ppermute(second, 'ta', ring('ta'))  1.06 us
  transfers between devices with their start and end apart: 7, of which 3 were waited for; matrix products, arithmetic and copies ran while one was open for 0% of the time, Pallas kernels for 24%

profile of v2, /device:TPU:0, one launch (start us, length us, event | category | flops | bytes accessed | tf_op | source)
XLA Modules:
  0.0 20.4 jit_solution(11636755349526105468)
XLA Ops:
  0.0 0.0 copy-start.1
  0.0 0.0 copy-start
  0.0 0.0 copy-start.4
  0.0 1.6 %shard_map.73 = (bf16[3,2,64,128]{3,2,1,0:T(8,128)(2,1)S(1)}, bf16[3,2,64,128]{3,2,1,0:T(8,128)(2,1)S(1)}, bf16[3,2,64,128]{3,2,1,0:T(8,128)(2,1)S(1)}, bf16[3,2...) custom-call(bf16[2,4,64,192]{3,2,1,0:T(8,128)(2,1)} %frames_hbm.1, bf16[2,4,64,192]{3,2,1,0:T(8,128)(2,1)} %cache_hbm.1, ...), custom_call_target="tpu_custom_call" | custom-call | flops 1000000000 | tf_op jit(solution)/shard_map/pallas_call | solution.py:361
  1.6 3.0 %collective-permute-start = (bf16[3,2,64,128]{3,2,1,0:T(8,128)(2,1)S(1)}, bf16[3,2,64,128]{3,2,1,0:T(8,128)(2,1)S(1)}, u32[]{:S(2)}, u32[]{:S(2)}) collective-permute-start(bf16[3,2,64,128]{3,2,1,0:T(8,128)(2,1)S(1)} %get-tuple-element.17), channel_id=1, source_target_pairs={{0,2},{2,0},{1,3},{3,1},{4,6},{6,4},{5,7},{7,5},{8,10},{10,8},{9,1... | collective-permute-start | bytes 294920 | tf_op jit(solution)/shard_map/ppermute | solution.py:387
  4.6 1.5 %collective-permute-start.2 = (bf16[3,2,64,128]{3,2,1,0:T(8,128)(2,1)S(1)}, bf16[3,2,64,128]{3,2,1,0:T(8,128)(2,1)S(1)}, u32[]{:S(2)}, u32[]{:S(2)}) collective-permute-start(bf16[3,2,64,128]{3,2,1,0:T(8,128)(2,1)S(1)} %get-tuple-element.18), channel_id=1, source_target_pairs={{0,6},{1,2},{2,4},{3,0},{4,10},{5,3},{6,8},{7,1},{8,14},{9,7},{10,... | collective-permute-start | bytes 294920 | tf_op jit(solution)/shard_map/ppermute | solution.py:389
  6.2 1.5 %collective-permute-start.1 = (bf16[3,2,64,128]{3,2,1,0:T(8,128)(2,1)S(1)}, bf16[3,2,64,128]{3,2,1,0:T(8,128)(2,1)S(1)}, u32[]{:S(2)}, u32[]{:S(2)}) collective-permute-start(bf16[3,2,64,128]{3,2,1,0:T(8,128)(2,1)S(1)} %get-tuple-element.18), channel_id=1, source_target_pairs={{0,2},{2,0},{1,3},{3,1},{4,6},{6,4},{5,7},{7,5},{8,10},{10,8},{9,1... | collective-permute-start | bytes 294920 | tf_op jit(solution)/shard_map/ppermute | solution.py:388
  7.7 1.6 %collective-permute-start.4 = (bf16[3,2,64,128]{3,2,1,0:T(8,128)(2,1)S(1)}, bf16[3,2,64,128]{3,2,1,0:T(8,128)(2,1)S(1)}, u32[]{:S(2)}, u32[]{:S(2)}) collective-permute-start(bf16[3,2,64,128]{3,2,1,0:T(8,128)(2,1)S(1)} %get-tuple-element.19.refs_6_.raw_first), channel_id=1, source_target_pairs={{0,4},{1,0},{2,6},{3,2},{4,8},{5,1},{6,10},{7,3},{8,12},{9,5},{10,... | collective-permute-start | bytes 294920 | tf_op jit(solution)/shard_map/ppermute | solution.py:390
  9.2 0.0 copy-start.2
  9.2 0.0 collective-permute-start.5
  9.2 0.0 collective-permute-done.refs_0_.main_a
  9.3 0.0 collective-permute-start.3
  9.3 0.0 copy-done.1
  9.3 0.2 shard_map.75.folded
  9.5 0.0 copy-done
  9.5 0.0 copy-done.4
  9.5 1.2 %shard_map.76 = (f32[2,6,64,192]{3,2,1,0:T(8,128)S(1)}, f32[2,8,192]{2,1,0:T(8,128)S(1)}) custom-call(bf16[3,2,64,128]{3,2,1,0:T(8,128)(2,1)S(1)} %get-tuple-element.19.refs_6_.raw_first, bf16[3,2,64,128]{3,2,1,0:T(8,128)(2,1)S(1)} %get-tuple-element.20.refs_7_.raw_second, bf16[2,4,64,192]{3,2,1,0:T(8,128)(2,1)S(1)} %get-tuple-element.21.act, ...), custom_call_target="tpu_custom_call" | custom-call | flops 1000000000 | tf_op jit(solution)/shard_map/pallas_call | solution.py:361
  10.7 0.0 copy-start.3
  10.8 0.0 collective-permute-done.2.refs_2_.prev_a
  10.8 1.1 %collective-permute-done.1.refs_1_.main_b = bf16[3,2,64,128]{3,2,1,0:T(8,128)(2,1)S(1)} collective-permute-done((bf16[3,2,64,128]{3,2,1,0:T(8,128)(2,1)S(1)}, bf16[3,2,64,128]{3,2,1,0:T(8,128)(2,1)S(1)}, u32[]{:S(2)}, u32[]{:S(2)}) %collective-permute-start.1) | collective-permute-done | bytes 98336 | tf_op jit(solution)/shard_map/ppermute | solution.py:388
  11.8 0.0 collective-permute-done.4.refs_4_.own_a
  11.8 2.0 %collective-permute-done.5.refs_5_.own_b = bf16[3,2,64,128]{3,2,1,0:T(8,128)(2,1)S(1)} collective-permute-done((bf16[3,2,64,128]{3,2,1,0:T(8,128)(2,1)S(1)}, bf16[3,2,64,128]{3,2,1,0:T(8,128)(2,1)S(1)}, u32[]{:S(2)}, u32[]{:S(2)}) %collective-permute-start.5) | collective-permute-done | bytes 98336 | tf_op jit(solution)/shard_map/ppermute | solution.py:391
  13.9 1.1 %collective-permute-done.3.refs_3_.prev_b = bf16[3,2,64,128]{3,2,1,0:T(8,128)(2,1)S(1)} collective-permute-done((bf16[3,2,64,128]{3,2,1,0:T(8,128)(2,1)S(1)}, bf16[3,2,64,128]{3,2,1,0:T(8,128)(2,1)S(1)}, u32[]{:S(2)}, u32[]{:S(2)}) %collective-permute-start.3) | collective-permute-done | bytes 98336 | tf_op jit(solution)/shard_map/ppermute | solution.py:392
  15.0 0.1 collective-permute-start.6
  15.1 0.0 copy-done.2
  15.1 1.9 %shard_map.77 = (f32[2,6,64,192]{3,2,1,0:T(8,128)S(1)}, f32[2,8,192]{2,1,0:T(8,128)S(1)}) custom-call(bf16[3,2,64,128]{3,2,1,0:T(8,128)(2,1)S(1)} %collective-permute-done.refs_0_.main_a, bf16[3,2,64,128]{3,2,1,0:T(8,128)(2,1)S(1)} %collective-permute-done.1.refs_1_.main_b, bf16[3,2,64,128]{3,2,1,0:T(8,128)(2,1)S(1)} %collective-permute-done.4.refs_4_.own_a, ...), custom_call_target="tpu_custom_call" | custom-call | flops 1000000000 | tf_op jit(solution)/shard_map/pallas_call | solution.py:361
  17.1 0.0 copy-done.3
  17.1 1.5 %shard_map.78 = (f32[2,6,8,192]{3,2,1,0:T(8,128)S(1)}, f32[2,8,192]{2,1,0:T(8,128)S(1)}, bf16[2,8,64,192]{3,2,1,0:T(8,128)(2,1)S(1)}) custom-call(bf16[3,2,64,128]{3,2,1,0:T(8,128)(2,1)S(1)} %collective-permute-done.2.refs_2_.prev_a, bf16[3,2,64,128]{3,2,1,0:T(8,128)(2,1)S(1)} %collective-permute-done.3.refs_3_.prev_b, ...), custom_call_target="tpu_custom_call" | custom-call | flops 1000000000 | tf_op jit(solution)/shard_map/pallas_call | solution.py:361
  18.5 0.0 collective-permute-done.6.sib
  18.5 1.9 %shard_map.79 = bf16[2,8,64,192]{3,2,1,0:T(8,128)(2,1)} custom-call(bf16[3,16,8,128]{3,2,1,0:T(8,128)(2,1)S(1)} %collective-permute-done.6.sib, bf16[3,3,3,192,192]{4,3,2,1,0:T(8,128)(2,1)S(1)} %copy-done, f32[2,6,8,192]{3,2,1,0:T(8,128)S(1)} %get-tuple-element.26.block_in, f32[2,8,192]{2,1,0:T(8,128)S(1)} %get-tuple-element.27.edge_in, ...), custom_call_target="tpu_custom_call" | custom-call | flops 1000000000 | tf_op jit(solution)/shard_map/pallas_call | solution.py:361
  (1 shorter events, 0.0 us)
Async XLA Ops:
  0.0 9.3 %copy-start.1 = (bf16[3,3,192,96]{3,2,1,0:T(8,128)(2,1)S(1)}, bf16[3,3,192,96]{3,2,1,0:T(8,128)(2,1)}, u32[]{:S(2)}) copy-start(bf16[3,3,192,96]{3,2,1,0:T(8,128)(2,1)} %weight.5) | copy-start | bytes 995332
  0.0 9.5 %copy-start = (bf16[3,3,3,192,192]{4,3,2,1,0:T(8,128)(2,1)S(1)}, bf16[3,3,3,192,192]{4,3,2,1,0:T(8,128)(2,1)}, u32[]{:S(2)}) copy-start(bf16[3,3,3,192,192]{4,3,2,1,0:T(8,128)(2,1)} %weight.9) | copy-start | bytes 5971972
  0.0 9.5 %copy-start.4 = (f32[192]{0:T(256)S(1)}, f32[192]{0:T(256)}, u32[]{:S(2)}) copy-start(f32[192]{0:T(256)} %bias.3) | copy-start | bytes 2308
  1.6 7.7 %collective-permute-start = (bf16[3,2,64,128]{3,2,1,0:T(8,128)(2,1)S(1)}, bf16[3,2,64,128]{3,2,1,0:T(8,128)(2,1)S(1)}, u32[]{:S(2)}, u32[]{:S(2)}) collective-permute-start(bf16[3,2,64,128]{3,2,1,0:T(8,128)(2,1)S(1)} %get-tuple-element.17), channel_id=1, source_target_pairs={{0,2},{2,0},{1,3},{3,1},{4,6},{6,4},{5,7},{7,5},{8,10},{10,8},{9,1... | collective-permute-start | bytes 294920 | tf_op jit(solution)/shard_map/ppermute | solution.py:387
  4.6 6.1 %collective-permute-start.2 = (bf16[3,2,64,128]{3,2,1,0:T(8,128)(2,1)S(1)}, bf16[3,2,64,128]{3,2,1,0:T(8,128)(2,1)S(1)}, u32[]{:S(2)}, u32[]{:S(2)}) collective-permute-start(bf16[3,2,64,128]{3,2,1,0:T(8,128)(2,1)S(1)} %get-tuple-element.18), channel_id=1, source_target_pairs={{0,6},{1,2},{2,4},{3,0},{4,10},{5,3},{6,8},{7,1},{8,14},{9,7},{10,... | collective-permute-start | bytes 294920 | tf_op jit(solution)/shard_map/ppermute | solution.py:389
  6.2 5.7 %collective-permute-start.1 = (bf16[3,2,64,128]{3,2,1,0:T(8,128)(2,1)S(1)}, bf16[3,2,64,128]{3,2,1,0:T(8,128)(2,1)S(1)}, u32[]{:S(2)}, u32[]{:S(2)}) collective-permute-start(bf16[3,2,64,128]{3,2,1,0:T(8,128)(2,1)S(1)} %get-tuple-element.18), channel_id=1, source_target_pairs={{0,2},{2,0},{1,3},{3,1},{4,6},{6,4},{5,7},{7,5},{8,10},{10,8},{9,1... | collective-permute-start | bytes 294920 | tf_op jit(solution)/shard_map/ppermute | solution.py:388
  7.7 4.2 %collective-permute-start.4 = (bf16[3,2,64,128]{3,2,1,0:T(8,128)(2,1)S(1)}, bf16[3,2,64,128]{3,2,1,0:T(8,128)(2,1)S(1)}, u32[]{:S(2)}, u32[]{:S(2)}) collective-permute-start(bf16[3,2,64,128]{3,2,1,0:T(8,128)(2,1)S(1)} %get-tuple-element.19.refs_6_.raw_first), channel_id=1, source_target_pairs={{0,4},{1,0},{2,6},{3,2},{4,8},{5,1},{6,10},{7,3},{8,12},{9,5},{10,... | collective-permute-start | bytes 294920 | tf_op jit(solution)/shard_map/ppermute | solution.py:390
  9.2 5.9 %copy-start.2 = (f32[192]{0:T(256)S(1)}, f32[192]{0:T(256)}, u32[]{:S(2)}) copy-start(f32[192]{0:T(256)} %gain.3) | copy-start | bytes 2308
  9.2 4.6 %collective-permute-start.5 = (bf16[3,2,64,128]{3,2,1,0:T(8,128)(2,1)S(1)}, bf16[3,2,64,128]{3,2,1,0:T(8,128)(2,1)S(1)}, u32[]{:S(2)}, u32[]{:S(2)}) collective-permute-start(bf16[3,2,64,128]{3,2,1,0:T(8,128)(2,1)S(1)} %get-tuple-element.20.refs_7_.raw_second), channel_id=1, source_target_pairs={{0,1},{1,5},{2,3},{3,7},{4,0},{5,9},{6,2},{7,11},{8,4},{9,13},{10,... | collective-permute-start | bytes 294920 | tf_op jit(solution)/shard_map/ppermute | solution.py:391
  9.3 5.7 %collective-permute-start.3 = (bf16[3,2,64,128]{3,2,1,0:T(8,128)(2,1)S(1)}, bf16[3,2,64,128]{3,2,1,0:T(8,128)(2,1)S(1)}, u32[]{:S(2)}, u32[]{:S(2)}) collective-permute-start(bf16[3,2,64,128]{3,2,1,0:T(8,128)(2,1)S(1)} %collective-permute-done.refs_0_.main_a), channel_id=1, source_target_pairs={{0,1},{1,5},{2,3},{3,7},{4,0},{5,9},{6,2},{7,11},{8,4},{9,13},{10,... | collective-permute-start | bytes 294920 | tf_op jit(solution)/shard_map/ppermute | solution.py:392
  10.7 6.3 %copy-start.3 = (f32[96]{0:T(128)S(1)}, f32[96]{0:T(128)}, u32[]{:S(2)}) copy-start(f32[96]{0:T(128)} %up_bias.3) | copy-start | bytes 1156
  15.0 3.5 %collective-permute-start.6 = (bf16[3,16,8,128]{3,2,1,0:T(8,128)(2,1)S(1)}, bf16[3,16,8,128]{3,2,1,0:T(8,128)(2,1)S(1)}, u32[]{:S(2)}, u32[]{:S(2)}) collective-permute-start(bf16[3,16,8,128]{3,2,1,0:T(8,128)(2,1)S(1)} %shard_map.74), channel_id=1, source_target_pairs={{0,1},{1,0},{2,3},{3,2},{4,5},{5,4},{6,7},{7,6},{8,9},{9,8},{10,11... | collective-permute-start | bytes 294920 | tf_op jit(solution)/shard_map/ppermute | solution.py:397

commit v3 on v2

--- a/solution.py
+++ b/solution.py
@@ -11,7 +11,7 @@
 EPS = 1e-06
 HALO = 2
 LANES = 128
-COST = 10**9
+COST = 8 * 10**8
 BLOCK = 8
 SUBLANES = 8
 AXES = ("ha", "ta", "wa")
@@ -58,13 +58,18 @@
                 frames, cache, gain, arrived):
     left = lax.axis_index("wa") == 0
     last = lax.axis_index("ta") == lax.axis_size("ta") - 1
-    copies = fetch((gain_hbm, frames_hbm, cache_hbm), (gain, frames, cache), arrived)
-    for copy in copies[:2]:
+    rows = frames.shape[1]
+    pieces = [(f, r) for f in range(frames.shape[0]) for r in range(rows)]
+    sources = [gain_hbm] + [frames_hbm.at[f, r] for f, r in pieces] + [cache_hbm.at[f, r] for f, r in pieces]
+    targets = [gain] + [frames.at[f, r] for f, r in pieces] + [cache.at[f, r] for f, r in pieces]
+    copies = fetch(sources, targets, arrived)
+    for copy in copies[: 1 + len(pieces)]:
         copy.wait()
     cells = frames[...]
     active = activate(cells, gain[...].reshape(1, -1)).astype(jnp.bfloat16)
     act[...] = active
-    copies[2].wait()
+    for copy in copies[1 + len(pieces) :]:
+        copy.wait()
     sent = packed(jnp.where(last, cache[...], active))
     first[...] = jnp.where(left, sent[:, :HALO], sent[:, HALO:])
     second[...] = jnp.where(left, sent[:, HALO:], sent[:, :HALO])
@@ -381,7 +386,7 @@
     first, second, raw_first, raw_second, act = call(
         pack_kernel, [HBM] * 3, (part, part, part, part, shape(frames.shape, bf16)),
         (pltpu.VMEM(frames.shape, bf16), pltpu.VMEM(cache.shape, bf16), pltpu.VMEM(norm_gain.shape, f32),
-         pltpu.SemaphoreType.DMA((3,))),
+         pltpu.SemaphoreType.DMA((1 + 2 * count * rows,))),
         COST, frames, cache, norm_gain,
     )
     main_a = lax.ppermute(first, "ta", ring("ta"))
@@ -409,7 +414,7 @@
         second_kernel, [VMEM] * 8, (body_shape, edge_shape), (tile, halo, halo, shift, shift),
         10**9, main_a, main_b, own_a, own_b, conv_weight, norm_gain, body, edge,
     )
-    folded = call(fold_kernel, [VMEM], shape((8, channels, 2 * outputs), bf16), (), 10**8, up_weight)
+    folded = call(fold_kernel, [VMEM], shape((8, channels, 2 * outputs), bf16), (), 3 * 10**9, up_weight)
     out_shape = (count, 2 * rows, cols, 2 * outputs)
     block, edge, out = call(
         third_kernel, [VMEM] * 7,

time: 20.5 us -> 20.5 us (level)
  waiting for transfers between devices: 4.23 us -> 2.75 us
  local copies, waits for them, and re-layouts: 0.02 us -> 1.5 us
    unnamed x10, local copies, waits for them, and re-layouts: 0.02 us -> 1.5 us
    ppermute x1, waiting for transfers between devices: 1.06 us -> 0.01 us  [block(): main_b = lax.ppermute(second, 'ta', ring('ta'))]
    ppermute x1, waiting for transfers between devices: 2.03 us -> 1.61 us  [block(): own_b = lax.ppermute(raw_second, AXES, against)]
  transfers between devices with their start and end apart: 7 -> 7, of which waited for: 3 -> 2; matrix products, arithmetic and copies ran while one was open for 0% -> 0% of each run, Pallas kernels for 24% -> 24%
where the time goes in v3:
time: 20.5 us; the launch traced here: 20.4 us
  Pallas kernels  8.23 us (40%)
  starting transfers between devices  7.74 us (38%)
  waiting for transfers between devices  2.75 us (13%)
  local copies, waits for them, and re-layouts  1.5 us (7%)
    pallas_call x7, Pallas kernels, call(): pl.pallas_call(kernel, out_shape=shapes, in_specs=specs, out_specs=jax.tr...  8.23 us
    ppermute x1, starting transfers between devices, block(): main_a = lax.ppermute(first, 'ta', ring('ta'))  3.03 us
    ppermute x1, waiting for transfers between devices, block(): own_b = lax.ppermute(raw_second, AXES, against)  1.61 us
    ppermute x1, starting transfers between devices, block(): own_a = lax.ppermute(raw_first, AXES, along)  1.58 us
    ppermute x1, starting transfers between devices, block(): prev_a = lax.ppermute(second, AXES, later)  1.55 us
    unnamed x10, local copies, waits for them, and re-layouts  1.5 us
    ppermute x1, starting transfers between devices, block(): main_b = lax.ppermute(second, 'ta', ring('ta'))  1.49 us
    ppermute x1, waiting for transfers between devices, block(): prev_b = lax.ppermute(main_a, AXES, against)  1.13 us
  transfers between devices with their start and end apart: 7, of which 2 were waited for; matrix products, arithmetic and copies ran while one was open for 0% of the time, Pallas kernels for 24%

profile of v3, /device:TPU:0, one launch (start us, length us, event | category | flops | bytes accessed | tf_op | source)
XLA Modules:
  0.0 20.4 jit_solution(16078802161896262647)
XLA Ops:
  0.0 0.0 copy-start.4
  0.0 1.5 %shard_map.73 = (bf16[3,2,64,128]{3,2,1,0:T(8,128)(2,1)S(1)}, bf16[3,2,64,128]{3,2,1,0:T(8,128)(2,1)S(1)}, bf16[3,2,64,128]{3,2,1,0:T(8,128)(2,1)S(1)}, bf16[3,2...) custom-call(bf16[2,4,64,192]{3,2,1,0:T(8,128)(2,1)} %frames_hbm.1, bf16[2,4,64,192]{3,2,1,0:T(8,128)(2,1)} %cache_hbm.1, ...), custom_call_target="tpu_custom_call" | custom-call | flops 800000000 | tf_op jit(solution)/shard_map/pallas_call | solution.py:366
  1.5 3.0 %collective-permute-start = (bf16[3,2,64,128]{3,2,1,0:T(8,128)(2,1)S(1)}, bf16[3,2,64,128]{3,2,1,0:T(8,128)(2,1)S(1)}, u32[]{:S(2)}, u32[]{:S(2)}) collective-permute-start(bf16[3,2,64,128]{3,2,1,0:T(8,128)(2,1)S(1)} %get-tuple-element.17), channel_id=1, source_target_pairs={{0,2},{2,0},{1,3},{3,1},{4,6},{6,4},{5,7},{7,5},{8,10},{10,8},{9,1... | collective-permute-start | bytes 294920 | tf_op jit(solution)/shard_map/ppermute | solution.py:392
  4.6 1.5 %collective-permute-start.2 = (bf16[3,2,64,128]{3,2,1,0:T(8,128)(2,1)S(1)}, bf16[3,2,64,128]{3,2,1,0:T(8,128)(2,1)S(1)}, u32[]{:S(2)}, u32[]{:S(2)}) collective-permute-start(bf16[3,2,64,128]{3,2,1,0:T(8,128)(2,1)S(1)} %get-tuple-element.18), channel_id=1, source_target_pairs={{0,6},{1,2},{2,4},{3,0},{4,10},{5,3},{6,8},{7,1},{8,14},{9,7},{10,... | collective-permute-start | bytes 294920 | tf_op jit(solution)/shard_map/ppermute | solution.py:394
  6.1 1.5 %collective-permute-start.1 = (bf16[3,2,64,128]{3,2,1,0:T(8,128)(2,1)S(1)}, bf16[3,2,64,128]{3,2,1,0:T(8,128)(2,1)S(1)}, u32[]{:S(2)}, u32[]{:S(2)}) collective-permute-start(bf16[3,2,64,128]{3,2,1,0:T(8,128)(2,1)S(1)} %get-tuple-element.18), channel_id=1, source_target_pairs={{0,2},{2,0},{1,3},{3,1},{4,6},{6,4},{5,7},{7,5},{8,10},{10,8},{9,1... | collective-permute-start | bytes 294920 | tf_op jit(solution)/shard_map/ppermute | solution.py:393
  7.6 1.6 %collective-permute-start.4 = (bf16[3,2,64,128]{3,2,1,0:T(8,128)(2,1)S(1)}, bf16[3,2,64,128]{3,2,1,0:T(8,128)(2,1)S(1)}, u32[]{:S(2)}, u32[]{:S(2)}) collective-permute-start(bf16[3,2,64,128]{3,2,1,0:T(8,128)(2,1)S(1)} %get-tuple-element.19.refs_6_.raw_first), channel_id=1, source_target_pairs={{0,4},{1,0},{2,6},{3,2},{4,8},{5,1},{6,10},{7,3},{8,12},{9,5},{10,... | collective-permute-start | bytes 294920 | tf_op jit(solution)/shard_map/ppermute | solution.py:395
  9.2 0.0 copy-start
  9.2 0.0 copy-start.3
  9.2 0.0 collective-permute-start.5
  9.2 0.0 collective-permute-done.refs_0_.main_a
  9.2 0.0 collective-permute-start.3
  9.2 0.0 copy-done.4
  9.2 0.2 %shard_map.75.folded = bf16[8,192,192]{2,1,0:T(8,128)(2,1)S(1)} custom-call(bf16[3,3,192,96]{3,2,1,0:T(8,128)(2,1)S(1)} %copy-done.4), custom_call_target="tpu_custom_call" | custom-call | flops 3000000000 | tf_op jit(solution)/shard_map/pallas_call | solution.py:366
  9.4 0.0 copy-start.1
  9.5 1.5 %copy-done = bf16[3,3,3,192,192]{4,3,2,1,0:T(8,128)(2,1)S(1)} copy-done((bf16[3,3,3,192,192]{4,3,2,1,0:T(8,128)(2,1)S(1)}, bf16[3,3,3,192,192]{4,3,2,1,0:T(8,128)(2,1)}, u32[]{:S(2)}) %copy-start) | copy-done | bytes 1990680
  10.9 0.0 copy-done.3
  10.9 1.2 %shard_map.76 = (f32[2,6,64,192]{3,2,1,0:T(8,128)S(1)}, f32[2,8,192]{2,1,0:T(8,128)S(1)}) custom-call(bf16[3,2,64,128]{3,2,1,0:T(8,128)(2,1)S(1)} %get-tuple-element.19.refs_6_.raw_first, bf16[3,2,64,128]{3,2,1,0:T(8,128)(2,1)S(1)} %get-tuple-element.20.refs_7_.raw_second, bf16[2,4,64,192]{3,2,1,0:T(8,128)(2,1)S(1)} %get-tuple-element.21.act, ...), custom_call_target="tpu_custom_call" | custom-call | flops 1000000000 | tf_op jit(solution)/shard_map/pallas_call | solution.py:366
  12.2 0.0 copy-start.2
  12.2 0.0 collective-permute-done.2.refs_2_.prev_a
  12.2 0.0 collective-permute-done.1.refs_1_.main_b
  12.2 0.0 collective-permute-done.4.refs_4_.own_a
  12.2 1.6 %collective-permute-done.5.refs_5_.own_b = bf16[3,2,64,128]{3,2,1,0:T(8,128)(2,1)S(1)} collective-permute-done((bf16[3,2,64,128]{3,2,1,0:T(8,128)(2,1)S(1)}, bf16[3,2,64,128]{3,2,1,0:T(8,128)(2,1)S(1)}, u32[]{:S(2)}, u32[]{:S(2)}) %collective-permute-start.5) | collective-permute-done | bytes 98336 | tf_op jit(solution)/shard_map/ppermute | solution.py:396
  13.8 1.1 %collective-permute-done.3.refs_3_.prev_b = bf16[3,2,64,128]{3,2,1,0:T(8,128)(2,1)S(1)} collective-permute-done((bf16[3,2,64,128]{3,2,1,0:T(8,128)(2,1)S(1)}, bf16[3,2,64,128]{3,2,1,0:T(8,128)(2,1)S(1)}, u32[]{:S(2)}, u32[]{:S(2)}) %collective-permute-start.3) | collective-permute-done | bytes 98336 | tf_op jit(solution)/shard_map/ppermute | solution.py:397
  15.0 0.1 collective-permute-start.6
  15.1 0.0 copy-done.1
  15.1 1.9 %shard_map.77 = (f32[2,6,64,192]{3,2,1,0:T(8,128)S(1)}, f32[2,8,192]{2,1,0:T(8,128)S(1)}) custom-call(bf16[3,2,64,128]{3,2,1,0:T(8,128)(2,1)S(1)} %collective-permute-done.refs_0_.main_a, bf16[3,2,64,128]{3,2,1,0:T(8,128)(2,1)S(1)} %collective-permute-done.1.refs_1_.main_b, bf16[3,2,64,128]{3,2,1,0:T(8,128)(2,1)S(1)} %collective-permute-done.4.refs_4_.own_a, ...), custom_call_target="tpu_custom_call" | custom-call | flops 1000000000 | tf_op jit(solution)/shard_map/pallas_call | solution.py:366
  17.0 0.0 copy-done.2
  17.0 1.5 %shard_map.78 = (f32[2,6,8,192]{3,2,1,0:T(8,128)S(1)}, f32[2,8,192]{2,1,0:T(8,128)S(1)}, bf16[2,8,64,192]{3,2,1,0:T(8,128)(2,1)S(1)}) custom-call(bf16[3,2,64,128]{3,2,1,0:T(8,128)(2,1)S(1)} %collective-permute-done.2.refs_2_.prev_a, bf16[3,2,64,128]{3,2,1,0:T(8,128)(2,1)S(1)} %collective-permute-done.3.refs_3_.prev_b, ...), custom_call_target="tpu_custom_call" | custom-call | flops 1000000000 | tf_op jit(solution)/shard_map/pallas_call | solution.py:366
  18.5 0.0 collective-permute-done.6.sib
  18.5 1.9 %shard_map.79 = bf16[2,8,64,192]{3,2,1,0:T(8,128)(2,1)} custom-call(bf16[3,16,8,128]{3,2,1,0:T(8,128)(2,1)S(1)} %collective-permute-done.6.sib, bf16[3,3,3,192,192]{4,3,2,1,0:T(8,128)(2,1)S(1)} %copy-done, f32[2,6,8,192]{3,2,1,0:T(8,128)S(1)} %get-tuple-element.26.block_in, f32[2,8,192]{2,1,0:T(8,128)S(1)} %get-tuple-element.27.edge_in, ...), custom_call_target="tpu_custom_call" | custom-call | flops 1000000000 | tf_op jit(solution)/shard_map/pallas_call | solution.py:366
  (1 shorter events, 0.0 us)
Async XLA Ops:
  0.0 9.2 %copy-start.4 = (bf16[3,3,192,96]{3,2,1,0:T(8,128)(2,1)S(1)}, bf16[3,3,192,96]{3,2,1,0:T(8,128)(2,1)}, u32[]{:S(2)}) copy-start(bf16[3,3,192,96]{3,2,1,0:T(8,128)(2,1)} %weight.5) | copy-start | bytes 995332
  1.5 7.7 %collective-permute-start = (bf16[3,2,64,128]{3,2,1,0:T(8,128)(2,1)S(1)}, bf16[3,2,64,128]{3,2,1,0:T(8,128)(2,1)S(1)}, u32[]{:S(2)}, u32[]{:S(2)}) collective-permute-start(bf16[3,2,64,128]{3,2,1,0:T(8,128)(2,1)S(1)} %get-tuple-element.17), channel_id=1, source_target_pairs={{0,2},{2,0},{1,3},{3,1},{4,6},{6,4},{5,7},{7,5},{8,10},{10,8},{9,1... | collective-permute-start | bytes 294920 | tf_op jit(solution)/shard_map/ppermute | solution.py:392
  4.6 7.6 %collective-permute-start.2 = (bf16[3,2,64,128]{3,2,1,0:T(8,128)(2,1)S(1)}, bf16[3,2,64,128]{3,2,1,0:T(8,128)(2,1)S(1)}, u32[]{:S(2)}, u32[]{:S(2)}) collective-permute-start(bf16[3,2,64,128]{3,2,1,0:T(8,128)(2,1)S(1)} %get-tuple-element.18), channel_id=1, source_target_pairs={{0,6},{1,2},{2,4},{3,0},{4,10},{5,3},{6,8},{7,1},{8,14},{9,7},{10,... | collective-permute-start | bytes 294920 | tf_op jit(solution)/shard_map/ppermute | solution.py:394
  6.1 6.1 %collective-permute-start.1 = (bf16[3,2,64,128]{3,2,1,0:T(8,128)(2,1)S(1)}, bf16[3,2,64,128]{3,2,1,0:T(8,128)(2,1)S(1)}, u32[]{:S(2)}, u32[]{:S(2)}) collective-permute-start(bf16[3,2,64,128]{3,2,1,0:T(8,128)(2,1)S(1)} %get-tuple-element.18), channel_id=1, source_target_pairs={{0,2},{2,0},{1,3},{3,1},{4,6},{6,4},{5,7},{7,5},{8,10},{10,8},{9,1... | collective-permute-start | bytes 294920 | tf_op jit(solution)/shard_map/ppermute | solution.py:393
  7.6 4.6 %collective-permute-start.4 = (bf16[3,2,64,128]{3,2,1,0:T(8,128)(2,1)S(1)}, bf16[3,2,64,128]{3,2,1,0:T(8,128)(2,1)S(1)}, u32[]{:S(2)}, u32[]{:S(2)}) collective-permute-start(bf16[3,2,64,128]{3,2,1,0:T(8,128)(2,1)S(1)} %get-tuple-element.19.refs_6_.raw_first), channel_id=1, source_target_pairs={{0,4},{1,0},{2,6},{3,2},{4,8},{5,1},{6,10},{7,3},{8,12},{9,5},{10,... | collective-permute-start | bytes 294920 | tf_op jit(solution)/shard_map/ppermute | solution.py:395
  9.2 1.7 %copy-start = (bf16[3,3,3,192,192]{4,3,2,1,0:T(8,128)(2,1)S(1)}, bf16[3,3,3,192,192]{4,3,2,1,0:T(8,128)(2,1)}, u32[]{:S(2)}) copy-start(bf16[3,3,3,192,192]{4,3,2,1,0:T(8,128)(2,1)} %weight.9) | copy-start | bytes 5971972
  9.2 1.8 %copy-start.3 = (f32[192]{0:T(256)S(1)}, f32[192]{0:T(256)}, u32[]{:S(2)}) copy-start(f32[192]{0:T(256)} %bias.3) | copy-start | bytes 2308
  9.2 4.6 %collective-permute-start.5 = (bf16[3,2,64,128]{3,2,1,0:T(8,128)(2,1)S(1)}, bf16[3,2,64,128]{3,2,1,0:T(8,128)(2,1)S(1)}, u32[]{:S(2)}, u32[]{:S(2)}) collective-permute-start(bf16[3,2,64,128]{3,2,1,0:T(8,128)(2,1)S(1)} %get-tuple-element.20.refs_7_.raw_second), channel_id=1, source_target_pairs={{0,1},{1,5},{2,3},{3,7},{4,0},{5,9},{6,2},{7,11},{8,4},{9,13},{10,... | collective-permute-start | bytes 294920 | tf_op jit(solution)/shard_map/ppermute | solution.py:396
  9.2 5.7 %collective-permute-start.3 = (bf16[3,2,64,128]{3,2,1,0:T(8,128)(2,1)S(1)}, bf16[3,2,64,128]{3,2,1,0:T(8,128)(2,1)S(1)}, u32[]{:S(2)}, u32[]{:S(2)}) collective-permute-start(bf16[3,2,64,128]{3,2,1,0:T(8,128)(2,1)S(1)} %collective-permute-done.refs_0_.main_a), channel_id=1, source_target_pairs={{0,1},{1,5},{2,3},{3,7},{4,0},{5,9},{6,2},{7,11},{8,4},{9,13},{10,... | collective-permute-start | bytes 294920 | tf_op jit(solution)/shard_map/ppermute | solution.py:397
  9.4 5.6 %copy-start.1 = (f32[192]{0:T(256)S(1)}, f32[192]{0:T(256)}, u32[]{:S(2)}) copy-start(f32[192]{0:T(256)} %gain.3) | copy-start | bytes 2308
  12.2 4.9 %copy-start.2 = (f32[96]{0:T(128)S(1)}, f32[96]{0:T(128)}, u32[]{:S(2)}) copy-start(f32[96]{0:T(128)} %up_bias.3) | copy-start | bytes 1156
  15.0 3.5 %collective-permute-start.6 = (bf16[3,16,8,128]{3,2,1,0:T(8,128)(2,1)S(1)}, bf16[3,16,8,128]{3,2,1,0:T(8,128)(2,1)S(1)}, u32[]{:S(2)}, u32[]{:S(2)}) collective-permute-start(bf16[3,16,8,128]{3,2,1,0:T(8,128)(2,1)S(1)} %shard_map.74), channel_id=1, source_target_pairs={{0,1},{1,0},{2,3},{3,2},{4,5},{5,4},{6,7},{7,6},{8,9},{9,8},{10,11... | collective-permute-start | bytes 294920 | tf_op jit(solution)/shard_map/ppermute | solution.py:402

commit v4 on v3

--- a/solution.py
+++ b/solution.py
@@ -244,15 +244,55 @@
                 out[t, 2 * r + p] = (total + line).astype(jnp.bfloat16)
 
 
-def edge_columns(near, edges, left):
-    frames, rows = near.shape[0], near.shape[1]
-    for f in range(frames):
-        for r in range(rows):
-            block = near[f, r].astype(jnp.float32)
+def edge_columns(near, rows, edges, left):
+    for f in range(near.shape[0]):
+        for i, r in enumerate(rows):
+            block = near[f, i].astype(jnp.float32)
             for s in range(HALO):
                 line = jnp.where(left, block[s : s + 1], block[BLOCK - 1 - s : BLOCK - s])
-                edges[f, s * rows + r : s * rows + r + 1, :] = line
-        edges[f, HALO * rows :, :] = jnp.zeros((SUBLANES, near.shape[-1]), jnp.float32)
+                edges[f, s * SUBLANES + r : s * SUBLANES + r + 1, :] = line
+
+
+def edge_sides(edges, f):
+    return [
+        jnp.concatenate([edges[f, b : b + SUBLANES], edges[f, SUBLANES + b : 2 * SUBLANES + b]], axis=0)
+        .astype(jnp.bfloat16)
+        for b in range(3)
+    ]
+
+
+def edge_sums(sides, a, weight):
+    sums = [None] * 3
+    for b in range(3):
+        window = jnp.concatenate([side[b] for side in sides], axis=0)
+        for c in range(3):
+            part = jnp.dot(window, weight[a, b, c], preferred_element_type=jnp.float32)
+            sums[c] = part if sums[c] is None else sums[c] + part
+    return sums
+
+
+def edge_kernel(sib, weight, gain, bias, sums_out, raw_out, near_prev, near_own, edges, raw):
+    left, core, top, bottom = place()
+    count = raw_out.shape[0]
+    rows = near_prev.shape[1]
+    far = rows + HALO
+    starts = (near_prev, (1 - core) * HALO), (near_prev, core * HALO), (near_own, (1 - core) * far), (near_own, core * far)
+    starts += (near_own, HALO + core * HALO), (near_own, HALO + (1 - core) * HALO)
+    for i, (cells, start) in enumerate(starts):
+        unpack(sib[:, i * HALO : (i + 1) * HALO], cells, start)
+    edges[...] = jnp.zeros(edges.shape, jnp.float32)
+    raw[...] = jnp.zeros(raw.shape, jnp.float32)
+    edge_columns(near_prev, range(HALO, far), edges.at[:2], left)
+    edge_columns(near_own, range(rows + 2 * HALO), raw, left)
+    inside = row_valid(2 * SUBLANES, SUBLANES, top, bottom, HALO)
+    for f in range(count):
+        value = activate(raw[f, : 2 * SUBLANES], gain[...].reshape(1, -1))
+        edges[2 + f, : 2 * SUBLANES] = jnp.where(inside, value, jnp.zeros_like(value))
+        raw_out[f] = raw[f, 1 : 1 + SUBLANES] + bias[...].reshape(1, -1)
+    sides = [edge_sides(edges, f) for f in range(2 + count)]
+    parts = [edge_sums(sides[a : a + count], a, weight) for a in range(3)]
+    for c in range(3):
+        sums_out[c] = parts[0][c] + parts[1][c] + parts[2][c]
 
 
 def near_kernel(*refs):
@@ -269,13 +309,12 @@
     return jnp.logical_not((top & (row < halo)) | (bottom & (row >= rows - halo)))
 
 
-def last_kernel(sib, weight, block_in, edge_in, folded, gain, bias, up_bias, done, out_hbm,
-                near_prev, near_own, edges, raw, wide, block, sent):
+def last_kernel(sib, weight, block_in, edge_in, sums_in, raw, folded, up_bias, done, out_hbm,
+                near_prev, edges, wide, block, sent):
     left, core, top, bottom = place()
     count, mid, _, channels = block_in.shape
     rows = mid - 2
     cols = done.shape[2]
-    far = rows + HALO
     rest = pl.ds(pl.multiple_of(core * BLOCK, BLOCK), cols - BLOCK)
     strip = pl.ds(pl.multiple_of((1 - core) * (cols - BLOCK), BLOCK), BLOCK)
     copies = [
@@ -283,40 +322,23 @@
     ]
     for copy in copies:
         copy.start()
-    starts = (HALO + (1 - core) * HALO, HALO + core * HALO, (1 - core) * far, core * far)
-    for i, start in enumerate(starts):
-        unpack(sib[:, i * HALO : (i + 1) * HALO], near_prev, start)
-    starts = ((1 - core) * far, core * far, HALO + core * HALO, HALO + (1 - core) * HALO)
-    for i, start in enumerate(starts):
-        unpack(sib[:, 4 * HALO + i * HALO : 4 * HALO + (i + 1) * HALO], near_own, start)
-    edge_columns(near_prev, edges.at[:2], left)
-    edge_columns(near_own, raw, left)
-    inside = row_valid(2 * SUBLANES, SUBLANES, top, bottom, HALO)
-    for f in range(2 + count):
-        value = edges[f, : 2 * SUBLANES] if f < 2 else activate(raw[f - 2, : 2 * SUBLANES], gain[...].reshape(1, -1))
-        edges[f, : 2 * SUBLANES] = jnp.where(inside, value, jnp.zeros_like(value))
-        edges[f, 2 * SUBLANES :] = jnp.zeros((SUBLANES, channels), jnp.float32)
-    sums = [None] * 3
-    for b in range(3):
-        side = [
-            jnp.concatenate([edges[f, b : b + SUBLANES], edges[f, SUBLANES + b : 2 * SUBLANES + b]], axis=0)
-            .astype(jnp.bfloat16)
-            for f in range(2 + count)
-        ]
-        for a in range(3):
-            window = jnp.concatenate(side[a : a + count], axis=0)
-            for c in range(3):
-                part = jnp.dot(window, weight[a, b, c], preferred_element_type=jnp.float32)
-                sums[c] = part if sums[c] is None else sums[c] + part
+    unpack(sib[:, :HALO], near_prev, (1 - core) * HALO)
+    unpack(sib[:, HALO:], near_prev, core * HALO)
+    clear_outside(near_prev, top, bottom)
+    edges[...] = jnp.zeros(edges.shape, jnp.float32)
+    edge_columns(near_prev, (*range(HALO), *range(HALO + rows, rows + 2 * HALO)), edges, left)
+    sides = [edge_sides(edges, f) for f in range(2)]
+    parts = [edge_sums(sides[a : a + count], a, weight) for a in range(2)]
     inside = row_valid(SUBLANES, mid, top, bottom, 1)
     row = lax.broadcasted_iota(jnp.int32, (SUBLANES, 1), 0)
     blank = jnp.zeros((SUBLANES, channels), jnp.float32)
     inner, rim = [], []
     for t in range(count):
-        near = [total[2 * SUBLANES * t : 2 * SUBLANES * t + SUBLANES] for total in sums]
-        next_ = [total[2 * SUBLANES * t + SUBLANES : 2 * SUBLANES * (t + 1)] for total in sums]
-        edge = edge_in[t] + near[1] + jnp.where(left, next_[2], next_[0])
-        edge = edge + raw[t, 1 : 1 + SUBLANES] + bias[...].reshape(1, -1)
+        span = slice(2 * SUBLANES * t, 2 * SUBLANES * (t + 1))
+        sums = [functools.reduce(jnp.add, [part[c][span] for part in parts[: 2 - t]], sums_in[c, span]) for c in range(3)]
+        near = [total[:SUBLANES] for total in sums]
+        next_ = [total[SUBLANES:] for total in sums]
+        edge = edge_in[t] + near[1] + jnp.where(left, next_[2], next_[0]) + raw[t]
         edges[t, :SUBLANES] = jnp.where(inside, edge, blank)
         rim.append(edges.at[t])
         lines = []
@@ -395,10 +417,10 @@
     own_a = lax.ppermute(raw_first, AXES, along)
     own_b = lax.ppermute(raw_second, AXES, against)
     prev_b = lax.ppermute(main_a, AXES, against)
-    sib = call(
-        near_kernel, [VMEM] * 8, shape((3, 4 * rows, BLOCK, LANES), bf16), (), 0,
-        main_a, main_b, prev_a, prev_b, own_a, own_b, raw_first, raw_second,
-    )
+    early = [main_a, main_b, own_a, own_b, raw_first, raw_second]
+    sib_early = call(near_kernel, [VMEM] * 6, shape((3, 6 * HALO, BLOCK, LANES), bf16), (), 0, *early)
+    sib_early = lax.ppermute(sib_early, "wa", sibling)
+    sib = call(near_kernel, [VMEM] * 2, shape((3, 2 * HALO, BLOCK, LANES), bf16), (), 0, prev_a, prev_b)
     sib = lax.ppermute(sib, "wa", sibling)
     mid, all_rows = rows + 2, rows + 2 * HALO
     body_shape = shape((count, mid, cols, channels), f32)
@@ -423,13 +445,18 @@
          pltpu.VMEM((2, rows, cols + 2 * SUBLANES, channels), f32)), 10**9,
         prev_a, prev_b, conv_weight, folded, up_bias, body, edge,
     )
-    near = pltpu.VMEM((2, all_rows, BLOCK, channels), bf16)
+    sums, raw = call(
+        edge_kernel, [VMEM] * 4, (shape((3, 2 * SUBLANES * count, channels), f32), edge_shape),
+        (pltpu.VMEM((2, rows, BLOCK, channels), bf16), pltpu.VMEM((count, all_rows, BLOCK, channels), bf16),
+         pltpu.VMEM((2 + count, 3 * SUBLANES, channels), f32), pltpu.VMEM((count, 3 * SUBLANES, channels), f32)),
+        10**9, sib_early, conv_weight, norm_gain, conv_bias,
+    )
     return call(
         last_kernel, [VMEM] * 9, shape(out_shape, bf16),
-        (near, near, pltpu.VMEM((2 + count, 3 * SUBLANES, channels), f32), pltpu.VMEM((count, 3 * SUBLANES, channels), f32),
+        (pltpu.VMEM((2, 2 * HALO, BLOCK, channels), bf16), pltpu.VMEM((2, 3 * SUBLANES, channels), f32),
          pltpu.VMEM((2, count * rows, BLOCK + 2 * SUBLANES, channels), f32),
          pltpu.VMEM((count, 2 * rows, BLOCK, 2 * outputs), bf16), pltpu.SemaphoreType.DMA((2 * count,))),
-        10**9, sib, conv_weight, block, edge, folded, norm_gain, conv_bias, up_bias, out, outs=HBM,
+        10**9, sib, conv_weight, block, edge, sums, raw, folded, up_bias, out, outs=HBM,
     )
 
 

time: 20.5 us -> 21.9 us (1.068)
  starting transfers between devices: 7.74 us -> 8.29 us
  waiting for transfers between devices: 2.75 us -> 3.16 us
  Pallas kernels: 8.23 us -> 8.58 us
    ppermute x1, starting transfers between devices: 3.03 us -> 1.49 us  [block(): main_a = lax.ppermute(first, 'ta', ring('ta'))]
    ppermute x1, starting transfers between devices: 1.49 us -> 3.03 us  [block(): main_b = lax.ppermute(second, 'ta', ring('ta'))]
    ppermute x1, starting transfers between devices: 0.02 us -> 0.5 us  [block(): prev_b = lax.ppermute(main_a, AXES, against)]
    ppermute x1, waiting for transfers between devices: 1.13 us -> 1.52 us  [block(): prev_b = lax.ppermute(main_a, AXES, against)]
    pallas_call x7 -> x9, Pallas kernels: 8.23 us -> 8.58 us  [call(): pl.pallas_call(kernel, out_shape=shapes, in_specs=specs, out_specs=jax.tr...]
  transfers between devices with their start and end apart: 7 -> 8, of which waited for: 2 -> 2; matrix products, arithmetic and copies ran while one was open for 0% -> 0% of each run, Pallas kernels for 24% -> 25%
where the time goes in v4:
time: 21.9 us; the launch traced here: 21.7 us
  Pallas kernels  8.58 us (39%)
  starting transfers between devices  8.29 us (38%)
  waiting for transfers between devices  3.16 us (14%)
  local copies, waits for them, and re-layouts  1.54 us (7%)
    pallas_call x9, Pallas kernels, call(): pl.pallas_call(kernel, out_shape=shapes, in_specs=specs, out_specs=jax.tr...  8.58 us
    ppermute x1, starting transfers between devices, block(): main_b = lax.ppermute(second, 'ta', ring('ta'))  3.03 us
    ppermute x1, waiting for transfers between devices, block(): own_b = lax.ppermute(raw_second, AXES, against)  1.62 us
    ppermute x1, starting transfers between devices, block(): own_a = lax.ppermute(raw_first, AXES, along)  1.58 us
    ppermute x1, starting transfers between devices, block(): prev_a = lax.ppermute(second, AXES, later)  1.55 us
    unnamed x10, local copies, waits for them, and re-layouts  1.54 us
    ppermute x1, waiting for transfers between devices, block(): prev_b = lax.ppermute(main_a, AXES, against)  1.52 us
    ppermute x1, starting transfers between devices, block(): main_a = lax.ppermute(first, 'ta', ring('ta'))  1.49 us
  transfers between devices with their start and end apart: 8, of which 2 were waited for; matrix products, arithmetic and copies ran while one was open for 0% of the time, Pallas kernels for 25%

profile of v4, /device:TPU:0, one launch (start us, length us, event | category | flops | bytes accessed | tf_op | source)
XLA Modules:
  0.0 21.7 jit_solution(9851120480438326308)
XLA Ops:
  0.0 0.0 copy-start.3
  0.0 1.5 %shard_map.73 = (bf16[3,2,64,128]{3,2,1,0:T(8,128)(2,1)S(1)}, bf16[3,2,64,128]{3,2,1,0:T(8,128)(2,1)S(1)}, bf16[3,2,64,128]{3,2,1,0:T(8,128)(2,1)S(1)}, bf16[3,2...) custom-call(bf16[2,4,64,192]{3,2,1,0:T(8,128)(2,1)} %frames_hbm.1, bf16[2,4,64,192]{3,2,1,0:T(8,128)(2,1)} %cache_hbm.1, ...), custom_call_target="tpu_custom_call" | custom-call | flops 800000000 | tf_op jit(solution)/shard_map/pallas_call | solution.py:388
  1.5 3.0 %collective-permute-start.4 = (bf16[3,2,64,128]{3,2,1,0:T(8,128)(2,1)S(1)}, bf16[3,2,64,128]{3,2,1,0:T(8,128)(2,1)S(1)}, u32[]{:S(2)}, u32[]{:S(2)}) collective-permute-start(bf16[3,2,64,128]{3,2,1,0:T(8,128)(2,1)S(1)} %get-tuple-element.19), channel_id=1, source_target_pairs={{0,2},{2,0},{1,3},{3,1},{4,6},{6,4},{5,7},{7,5},{8,10},{10,8},{9,1... | collective-permute-start | bytes 294920 | tf_op jit(solution)/shard_map/ppermute | solution.py:415
  4.6 1.5 %collective-permute-start = (bf16[3,2,64,128]{3,2,1,0:T(8,128)(2,1)S(1)}, bf16[3,2,64,128]{3,2,1,0:T(8,128)(2,1)S(1)}, u32[]{:S(2)}, u32[]{:S(2)}) collective-permute-start(bf16[3,2,64,128]{3,2,1,0:T(8,128)(2,1)S(1)} %get-tuple-element.19), channel_id=1, source_target_pairs={{0,6},{1,2},{2,4},{3,0},{4,10},{5,3},{6,8},{7,1},{8,14},{9,7},{10,... | collective-permute-start | bytes 294920 | tf_op jit(solution)/shard_map/ppermute | solution.py:416
  6.1 1.5 %collective-permute-start.1 = (bf16[3,2,64,128]{3,2,1,0:T(8,128)(2,1)S(1)}, bf16[3,2,64,128]{3,2,1,0:T(8,128)(2,1)S(1)}, u32[]{:S(2)}, u32[]{:S(2)}) collective-permute-start(bf16[3,2,64,128]{3,2,1,0:T(8,128)(2,1)S(1)} %get-tuple-element.20), channel_id=1, source_target_pairs={{0,2},{2,0},{1,3},{3,1},{4,6},{6,4},{5,7},{7,5},{8,10},{10,8},{9,1... | collective-permute-start | bytes 294920 | tf_op jit(solution)/shard_map/ppermute | solution.py:414
  7.6 1.6 %collective-permute-start.5 = (bf16[3,2,64,128]{3,2,1,0:T(8,128)(2,1)S(1)}, bf16[3,2,64,128]{3,2,1,0:T(8,128)(2,1)S(1)}, u32[]{:S(2)}, u32[]{:S(2)}) collective-permute-start(bf16[3,2,64,128]{3,2,1,0:T(8,128)(2,1)S(1)} %get-tuple-element.21.raw_first.refs_4_), channel_id=1, source_target_pairs={{0,4},{1,0},{2,6},{3,2},{4,8},{5,1},{6,10},{7,3},{8,12},{9,5},{10,... | collective-permute-start | bytes 294920 | tf_op jit(solution)/shard_map/ppermute | solution.py:417
  9.2 0.0 copy-start
  9.2 0.0 copy-start.4
  9.2 0.0 collective-permute-start.6
  9.2 0.0 copy-done.3
  9.2 0.2 shard_map.75.folded
  9.4 0.0 copy-start.2
  9.4 1.5 %copy-done = bf16[3,3,3,192,192]{4,3,2,1,0:T(8,128)(2,1)S(1)} copy-done((bf16[3,3,3,192,192]{4,3,2,1,0:T(8,128)(2,1)S(1)}, bf16[3,3,3,192,192]{4,3,2,1,0:T(8,128)(2,1)}, u32[]{:S(2)}) %copy-start) | copy-done | bytes 1990680
  10.9 0.0 copy-done.4
  10.9 1.2 %shard_map.76 = (f32[2,6,64,192]{3,2,1,0:T(8,128)S(1)}, f32[2,8,192]{2,1,0:T(8,128)S(1)}) custom-call(bf16[3,2,64,128]{3,2,1,0:T(8,128)(2,1)S(1)} %get-tuple-element.21.raw_first.refs_4_, bf16[3,2,64,128]{3,2,1,0:T(8,128)(2,1)S(1)} %get-tuple-element.22.raw_second.refs_5_, bf16[2,4,64,192]{3,2,1,0:T(8,128)(2,1)S(1)} %get-tuple-element.23.act, ...), custom_call_target="tpu_custom_call" | custom-call | flops 1000000000 | tf_op jit(solution)/shard_map/pallas_call | solution.py:388
  12.2 0.0 collective-permute-done.1.main_a.refs_0_
  12.2 0.0 collective-permute-done.4.main_b.refs_1_
  12.2 0.0 collective-permute-done.5.own_a.refs_2_
  12.2 1.6 %collective-permute-done.6.own_b.refs_3_ = bf16[3,2,64,128]{3,2,1,0:T(8,128)(2,1)S(1)} collective-permute-done((bf16[3,2,64,128]{3,2,1,0:T(8,128)(2,1)S(1)}, bf16[3,2,64,128]{3,2,1,0:T(8,128)(2,1)S(1)}, u32[]{:S(2)}, u32[]{:S(2)}) %collective-permute-start.6) | collective-permute-done | bytes 98336 | tf_op jit(solution)/shard_map/ppermute | solution.py:418
  13.8 0.1 collective-permute-start.7
  13.9 0.5 %collective-permute-start.2 = (bf16[3,2,64,128]{3,2,1,0:T(8,128)(2,1)S(1)}, bf16[3,2,64,128]{3,2,1,0:T(8,128)(2,1)S(1)}, u32[]{:S(2)}, u32[]{:S(2)}) collective-permute-start(bf16[3,2,64,128]{3,2,1,0:T(8,128)(2,1)S(1)} %collective-permute-done.1.main_a.refs_0_), channel_id=1, source_target_pairs={{0,1},{1,5},{2,3},{3,7},{4,0},{5,9},{6,2},{7,11},{8,4},{9,13},{10,... | collective-permute-start | bytes 294920 | tf_op jit(solution)/shard_map/ppermute | solution.py:419
  14.4 0.0 copy-done.2
  14.4 1.9 %shard_map.77 = (f32[2,6,64,192]{3,2,1,0:T(8,128)S(1)}, f32[2,8,192]{2,1,0:T(8,128)S(1)}) custom-call(bf16[3,2,64,128]{3,2,1,0:T(8,128)(2,1)S(1)} %collective-permute-done.1.main_a.refs_0_, bf16[3,2,64,128]{3,2,1,0:T(8,128)(2,1)S(1)} %collective-permute-done.4.main_b.refs_1_, bf16[3,2,64,128]{3,2,1,0:T(8,128)(2,1)S(1)} %collective-permute-done.5.own_a.refs_2_, ...), custom_call_target="tpu_custom_call" | custom-call | flops 1000000000 | tf_op jit(solution)/shard_map/pallas_call | solution.py:388
  16.4 0.0 copy-start.1
  16.4 0.0 collective-permute-done.7.sib
  16.4 0.6 %shard_map.80 = (f32[3,32,192]{2,1,0:T(8,128)S(1)}, f32[2,8,192]{2,1,0:T(8,128)S(1)}) custom-call(bf16[3,12,8,128]{3,2,1,0:T(8,128)(2,1)S(1)} %collective-permute-done.7.sib, bf16[3,3,3,192,192]{4,3,2,1,0:T(8,128)(2,1)S(1)} %copy-done, f32[192]{0:T(256)S(1)} %copy-done.2, f32[192]{0:T(256)S(1)} %copy-done.4), custom_call_target="tpu_custom_call" | custom-call | flops 1000000000 | tf_op jit(solution)/shard_map/pallas_call | solution.py:388
  17.0 0.0 collective-permute-done.refs_0_.prev_a
  17.0 1.5 %collective-permute-done.2.refs_1_.prev_b = bf16[3,2,64,128]{3,2,1,0:T(8,128)(2,1)S(1)} collective-permute-done((bf16[3,2,64,128]{3,2,1,0:T(8,128)(2,1)S(1)}, bf16[3,2,64,128]{3,2,1,0:T(8,128)(2,1)S(1)}, u32[]{:S(2)}, u32[]{:S(2)}) %collective-permute-start.2) | collective-permute-done | bytes 98336 | tf_op jit(solution)/shard_map/ppermute | solution.py:419
  18.6 0.1 collective-permute-start.3
  18.6 0.0 copy-done.1
  18.7 1.5 %shard_map.78 = (f32[2,6,8,192]{3,2,1,0:T(8,128)S(1)}, f32[2,8,192]{2,1,0:T(8,128)S(1)}, bf16[2,8,64,192]{3,2,1,0:T(8,128)(2,1)S(1)}) custom-call(bf16[3,2,64,128]{3,2,1,0:T(8,128)(2,1)S(1)} %collective-permute-done.refs_0_.prev_a, bf16[3,2,64,128]{3,2,1,0:T(8,128)(2,1)S(1)} %collective-permute-done.2.refs_1_.prev_b, ...), custom_call_target="tpu_custom_call" | custom-call | flops 1000000000 | tf_op jit(solution)/shard_map/pallas_call | solution.py:388
  20.1 0.0 collective-permute-done.3.sib
  20.1 1.6 %shard_map.81 = bf16[2,8,64,192]{3,2,1,0:T(8,128)(2,1)} custom-call(bf16[3,4,8,128]{3,2,1,0:T(8,128)(2,1)S(1)} %collective-permute-done.3.sib, bf16[3,3,3,192,192]{4,3,2,1,0:T(8,128)(2,1)S(1)} %copy-done, f32[2,6,8,192]{3,2,1,0:T(8,128)S(1)} %get-tuple-element.28.block_in, f32[2,8,192]{2,1,0:T(8,128)S(1)} %get-tuple-element.29.edge_in, ...), custom_call_target="tpu_custom_call" | custom-call | flops 1000000000 | tf_op jit(solution)/shard_map/pallas_call | solution.py:388
  (2 shorter events, 0.0 us)
Async XLA Ops:
  0.0 9.2 %copy-start.3 = (bf16[3,3,192,96]{3,2,1,0:T(8,128)(2,1)S(1)}, bf16[3,3,192,96]{3,2,1,0:T(8,128)(2,1)}, u32[]{:S(2)}) copy-start(bf16[3,3,192,96]{3,2,1,0:T(8,128)(2,1)} %weight.6) | copy-start | bytes 995332
  1.5 10.6 %collective-permute-start.4 = (bf16[3,2,64,128]{3,2,1,0:T(8,128)(2,1)S(1)}, bf16[3,2,64,128]{3,2,1,0:T(8,128)(2,1)S(1)}, u32[]{:S(2)}, u32[]{:S(2)}) collective-permute-start(bf16[3,2,64,128]{3,2,1,0:T(8,128)(2,1)S(1)} %get-tuple-element.19), channel_id=1, source_target_pairs={{0,2},{2,0},{1,3},{3,1},{4,6},{6,4},{5,7},{7,5},{8,10},{10,8},{9,1... | collective-permute-start | bytes 294920 | tf_op jit(solution)/shard_map/ppermute | solution.py:415
  4.6 12.5 %collective-permute-start = (bf16[3,2,64,128]{3,2,1,0:T(8,128)(2,1)S(1)}, bf16[3,2,64,128]{3,2,1,0:T(8,128)(2,1)S(1)}, u32[]{:S(2)}, u32[]{:S(2)}) collective-permute-start(bf16[3,2,64,128]{3,2,1,0:T(8,128)(2,1)S(1)} %get-tuple-element.19), channel_id=1, source_target_pairs={{0,6},{1,2},{2,4},{3,0},{4,10},{5,3},{6,8},{7,1},{8,14},{9,7},{10,... | collective-permute-start | bytes 294920 | tf_op jit(solution)/shard_map/ppermute | solution.py:416
  6.1 6.0 %collective-permute-start.1 = (bf16[3,2,64,128]{3,2,1,0:T(8,128)(2,1)S(1)}, bf16[3,2,64,128]{3,2,1,0:T(8,128)(2,1)S(1)}, u32[]{:S(2)}, u32[]{:S(2)}) collective-permute-start(bf16[3,2,64,128]{3,2,1,0:T(8,128)(2,1)S(1)} %get-tuple-element.20), channel_id=1, source_target_pairs={{0,2},{2,0},{1,3},{3,1},{4,6},{6,4},{5,7},{7,5},{8,10},{10,8},{9,1... | collective-permute-start | bytes 294920 | tf_op jit(solution)/shard_map/ppermute | solution.py:414
  7.6 4.6 %collective-permute-start.5 = (bf16[3,2,64,128]{3,2,1,0:T(8,128)(2,1)S(1)}, bf16[3,2,64,128]{3,2,1,0:T(8,128)(2,1)S(1)}, u32[]{:S(2)}, u32[]{:S(2)}) collective-permute-start(bf16[3,2,64,128]{3,2,1,0:T(8,128)(2,1)S(1)} %get-tuple-element.21.raw_first.refs_4_), channel_id=1, source_target_pairs={{0,4},{1,0},{2,6},{3,2},{4,8},{5,1},{6,10},{7,3},{8,12},{9,5},{10,... | collective-permute-start | bytes 294920 | tf_op jit(solution)/shard_map/ppermute | solution.py:417
  9.2 1.7 %copy-start = (bf16[3,3,3,192,192]{4,3,2,1,0:T(8,128)(2,1)S(1)}, bf16[3,3,3,192,192]{4,3,2,1,0:T(8,128)(2,1)}, u32[]{:S(2)}) copy-start(bf16[3,3,3,192,192]{4,3,2,1,0:T(8,128)(2,1)} %weight.11) | copy-start | bytes 5971972
  9.2 1.8 %copy-start.4 = (f32[192]{0:T(256)S(1)}, f32[192]{0:T(256)}, u32[]{:S(2)}) copy-start(f32[192]{0:T(256)} %bias.3) | copy-start | bytes 2308
  9.2 4.6 %collective-permute-start.6 = (bf16[3,2,64,128]{3,2,1,0:T(8,128)(2,1)S(1)}, bf16[3,2,64,128]{3,2,1,0:T(8,128)(2,1)S(1)}, u32[]{:S(2)}, u32[]{:S(2)}) collective-permute-start(bf16[3,2,64,128]{3,2,1,0:T(8,128)(2,1)S(1)} %get-tuple-element.22.raw_second.refs_5_), channel_id=1, source_target_pairs={{0,1},{1,5},{2,3},{3,7},{4,0},{5,9},{6,2},{7,11},{8,4},{9,13},{10,... | collective-permute-start | bytes 294920 | tf_op jit(solution)/shard_map/ppermute | solution.py:418
  9.4 5.0 %copy-start.2 = (f32[192]{0:T(256)S(1)}, f32[192]{0:T(256)}, u32[]{:S(2)}) copy-start(f32[192]{0:T(256)} %gain.3) | copy-start | bytes 2308
  13.8 2.5 %collective-permute-start.7 = (bf16[3,12,8,128]{3,2,1,0:T(8,128)(2,1)S(1)}, bf16[3,12,8,128]{3,2,1,0:T(8,128)(2,1)S(1)}, u32[]{:S(2)}, u32[]{:S(2)}) collective-permute-start(bf16[3,12,8,128]{3,2,1,0:T(8,128)(2,1)S(1)} %shard_map.79), channel_id=1, source_target_pairs={{0,1},{1,0},{2,3},{3,2},{4,5},{5,4},{6,7},{7,6},{8,9},{9,8},{10,11... | collective-permute-start | bytes 221192 | tf_op jit(solution)/shard_map/ppermute | solution.py:422
  13.9 4.6 %collective-permute-start.2 = (bf16[3,2,64,128]{3,2,1,0:T(8,128)(2,1)S(1)}, bf16[3,2,64,128]{3,2,1,0:T(8,128)(2,1)S(1)}, u32[]{:S(2)}, u32[]{:S(2)}) collective-permute-start(bf16[3,2,64,128]{3,2,1,0:T(8,128)(2,1)S(1)} %collective-permute-done.1.main_a.refs_0_), channel_id=1, source_target_pairs={{0,1},{1,5},{2,3},{3,7},{4,0},{5,9},{6,2},{7,11},{8,4},{9,13},{10,... | collective-permute-start | bytes 294920 | tf_op jit(solution)/shard_map/ppermute | solution.py:419
  16.4 2.3 %copy-start.1 = (f32[96]{0:T(128)S(1)}, f32[96]{0:T(128)}, u32[]{:S(2)}) copy-start(f32[96]{0:T(128)} %up_bias.3) | copy-start | bytes 1156
  18.6 1.6 %collective-permute-start.3 = (bf16[3,4,8,128]{3,2,1,0:T(8,128)(2,1)S(1)}, bf16[3,4,8,128]{3,2,1,0:T(8,128)(2,1)S(1)}, u32[]{:S(2)}, u32[]{:S(2)}) collective-permute-start(bf16[3,4,8,128]{3,2,1,0:T(8,128)(2,1)S(1)} %shard_map.74), channel_id=1, source_target_pairs={{0,1},{1,0},{2,3},{3,2},{4,5},{5,4},{6,7},{7,6},{8,9},{9,8},{10,11... | collective-permute-start | bytes 73736 | tf_op jit(solution)/shard_map/ppermute | solution.py:424
